TPU v7x, 256 devices: a whole 4x4x8 slice. The times are simulated.
256 devices in a mesh: obs: 64 (over z, y, core), rep: 4 (over x).
Axes of the slice: x: 4, y: 4, z: 8, core: 2. Of those that a mesh axis runs over, the one named last changes fastest.
Arguments:
- jacobians: float32 [18, 8388608], P(None, ('obs', 'rep')), may hold values from -3 to 3
- residuals: float32 [2, 8388608], P(None, ('obs', 'rep')), may hold values from -6 to 6
- camera_local: int32 [8388608], P(('obs', 'rep')), may hold values from 0 to 1023
- bucket_counts: int32 [256, 64], P(('obs', 'rep')), may hold values from 1 to 512, as said below
- camera_map: int32 [65536], replicated, may hold values from 0 to 65535, each once
Outputs:
- gradient: float32 [9, 65536], replicated
- camera_blocks: float32 [81, 65536], P(None, 'obs')
Inputs may be any that keep to these rules, and one draw needn't show every extreme that they name: bucket_counts[s, d] counts the leading live slots of bucket d of source block s; exactly one destination d has all 512 slots live from every source block, and every other bucket has at most 256 live slots. A slot in bucket d names camera slot d * 1024 + camera_local. `camera_map`: each camera id appears once.
All inputs are finite; a program needn't handle non-finite values.
Results may differ from a plain program's by a relative error of at most 0.0003.
Values sent between devices are 32-bit elements; how exact they have to be, the bound alone decides.
A program may use at most 192 MiB of HBM per device.

v0:
```python
import functools

import jax
import jax.numpy as jnp
from jax import lax
from jax.experimental import pallas as pl
from jax.experimental.pallas import tpu as pltpu
from jax.sharding import PartitionSpec as P

CAM_DEV = 1024
MESH = pl.DeviceIdType.MESH
F32 = jnp.float32
BF16 = jnp.bfloat16
VMEM = pltpu.VMEM
ROWS = 56
HEAD = 16
KEPT = 48
LOW = 256


def vspec():
    return pl.BlockSpec(memory_space=VMEM)


def split(value):
    high = value.astype(BF16).astype(F32)
    return high, value - high


def pack(counts, jac, res, ids, out):
    buckets = counts.shape[1]
    cap = jac.shape[1] // buckets
    out[0:18, :] = jac[...]
    out[18:20, :] = res[...]
    place = lax.broadcasted_iota(jnp.int32, (1, cap), 1)
    for d in range(buckets):
        lanes = slice(d * cap, (d + 1) * cap)
        out[20:21, lanes] = jnp.where(place < counts[0, d], ids[:, lanes], -1).astype(F32)


def one_hot_of(low, wide):
    shape = (wide, low.shape[1])
    rows = lax.broadcasted_iota(jnp.int32, shape, 0).astype(F32).astype(BF16)
    there = jnp.broadcast_to(low.astype(F32), shape).astype(BF16)
    return jnp.where(there == rows, jnp.ones(shape, BF16), jnp.zeros(shape, BF16))


def add_block(block, terms, acc):
    cap = block.shape[1]
    lead, trail, res = block[0:9], block[9:18], block[18:20]
    ids = block[20:21].astype(jnp.int32)
    at = 9
    for k in range(9):
        terms[at : at + 9 - k, :] = lead[k : k + 1] * lead[k:9] + trail[k : k + 1] * trail[k:9]
        at += 9 - k
    terms[0:9, :] = lead * res[0:1] + trail * res[1:2]
    high, low = split(terms[...])
    both = jnp.concatenate([high, low], axis=0).astype(BF16)
    pieces, _, width = acc.shape
    up = jnp.where(ids < 0, -1, ids // width)
    down = ids - up * width
    one_hot = one_hot_of(down, width)
    up = jnp.broadcast_to(up.astype(F32), both.shape).astype(BF16)
    zero = jnp.zeros_like(both)
    lhs = jnp.concatenate([jnp.where(up == jnp.asarray(h, BF16), both, zero) for h in range(pieces)], axis=0)
    added = lax.dot_general(lhs, one_hot, (((1,), (1,)), ((), ())), preferred_element_type=F32)
    for h in range(pieces):
        at = h * 2 * ROWS
        acc[h] += added[at : at + ROWS] + added[at + ROWS : at + 2 * ROWS]


def expand(blocks, out):
    m, _, width = blocks.shape
    at = 1
    for k in range(9):
        for l in range(k, 9):
            for r in range(m):
                row = blocks[r, at : at + 1, :]
                lanes = slice(r * width, (r + 1) * width)
                out[k * 9 + l : k * 9 + l + 1, lanes] = row
                if l != k:
                    out[l * 9 + k : l * 9 + k + 1, lanes] = row
            at += 1


def place_chunk(o, grads, cmap, ready, acc):
    m, n, _, width = grads.shape
    span = m * width
    highs = n * span // LOW
    slots = jnp.concatenate([grads[r, o] for r in range(m)], axis=1)
    ids = cmap[:, pl.ds(pl.multiple_of(o * span, span), span)]
    up = ids // LOW
    one_hot = one_hot_of(lax.rem(ids, LOW), LOW) if ready is None else ready[o]
    high, low = split(slots)
    top = jnp.concatenate([high[0:8], low[0:8]], axis=0).astype(BF16)
    up16 = jnp.broadcast_to(up.astype(F32), (16, span)).astype(BF16)
    none = jnp.zeros_like(top)
    mask = up == lax.broadcasted_iota(jnp.int32, (highs, span), 0)
    last = jnp.concatenate([jnp.where(mask, high[8:9], 0.0), jnp.where(mask, low[8:9], 0.0)], axis=0).astype(BF16)
    dims = (((1,), (1,)), ((), ()))
    group = min(highs, 32)

    def tiles(start):
        return [jnp.where(up16 == jnp.asarray(start + h, F32).astype(BF16), top, none) for h in range(group)]

    if group == highs:
        lhs = jnp.concatenate(tiles(0) + [last], axis=0)
        acc[...] += lax.dot_general(lhs, one_hot, dims, preferred_element_type=F32)
        return

    def some(g, carry):
        lhs = jnp.concatenate(tiles(g * group), axis=0)
        where = pl.ds(pl.multiple_of(g * group * 16, group * 16), group * 16)
        acc[where, :] += lax.dot_general(lhs, one_hot, dims, preferred_element_type=F32)
        return carry

    lax.fori_loop(0, highs // group, some, 0)
    acc[highs * 16 :, :] += lax.dot_general(last, one_hot, dims, preferred_element_type=F32)


def lay_out(acc, gradient):
    highs = gradient.shape[1] // LOW
    for h in range(highs):
        lanes = slice(h * LOW, (h + 1) * LOW)
        gradient[0:8, lanes] = acc[h * 16 : h * 16 + 8, :] + acc[h * 16 + 8 : h * 16 + 16, :]
        ninth = highs * 16 + h
        gradient[8:9, lanes] = acc[ninth : ninth + 1, :] + acc[ninth + highs : ninth + highs + 1, :]


def main_kernel(
    n, m, counts, jac_in, res_in, ids_in, cmap_in, gradient, out, jac, res, ids, cmap, load_sem, blocks, grads, ready, spread, packed, moved, terms, part, landed, total, mine,
    x_send, x_recv, a_send, a_recv, b_send, b_recv, g_send, g_recv, c_send, c_recv,
):
    me, rep = lax.axis_index("obs"), lax.axis_index("rep")
    width = total.shape[1]
    cap = moved.shape[2]
    barrier = pltpu.get_barrier_semaphore()
    for i in range(1, n):
        pl.semaphore_signal(barrier, inc=1, device_id={"obs": lax.rem(me + i, n)}, device_id_type=MESH)
    for i in range(1, m):
        pl.semaphore_signal(barrier, inc=1, device_id={"rep": lax.rem(rep + i, m)}, device_id_type=MESH)
    pairs = ((jac_in, jac), (res_in, res), (ids_in, ids), (cmap_in, cmap))
    loads = [pltpu.make_async_copy(src, dst, load_sem.at[k]) for k, (src, dst) in enumerate(pairs)]
    for load in loads:
        load.start()
    part[...] = jnp.zeros_like(part)
    terms[...] = jnp.zeros_like(terms)
    spread[...] = jnp.zeros_like(spread)
    for load in loads:
        load.wait()
    pack(counts, jac, res, ids, packed)
    pl.semaphore_wait(barrier, n + m - 2)

    def lanes_of(peer):
        return pl.ds(pl.multiple_of(peer * cap, cap), cap)

    def handing(i):
        peer = lax.rem(me + i, n)
        return pltpu.make_async_remote_copy(
            src_ref=packed.at[:, lanes_of(peer)],
            dst_ref=moved.at[i],
            send_sem=x_send.at[i],
            recv_sem=x_recv.at[i],
            device_id={"obs": peer},
            device_id_type=MESH,
        )

    def start(i, carry):
        handing(i).start()
        return carry

    def take(i, carry):
        handing(i).wait_recv()
        add_block(moved[i], terms, part)
        return carry

    def drain(i, carry):
        handing(i).wait_send()
        return carry

    lax.fori_loop(1, n, start, 0)
    add_block(packed[:, lanes_of(me)], terms, part)
    early = ready.shape[0] == n
    span = m * width

    def prepare(o, carry):
        ids_here = cmap[:, pl.ds(pl.multiple_of(o * span, span), span)]
        ready[o] = one_hot_of(lax.rem(ids_here, LOW), LOW)
        return carry

    if early:
        lax.fori_loop(0, n, prepare, 0)
    lax.fori_loop(1, n, take, 0)

    def send(src, dst, s, r, axis, peer):
        copy = pltpu.make_async_remote_copy(
            src_ref=src, dst_ref=dst, send_sem=s, recv_sem=r, device_id={axis: peer}, device_id_type=MESH
        )
        copy.start()
        return copy

    first, second = [], []
    for half, rows, copies in ((0, pl.ds(0, HEAD), first), (1, pl.ds(HEAD, ROWS - HEAD), second)):
        for i in range(1, m):
            peer = lax.rem(rep + i, m)
            copies.append(
                send(part.at[peer, rows], landed.at[i, rows], a_send.at[half, i], a_recv.at[half, i], "rep", peer)
            )
    for copy in first:
        copy.wait_recv()
    head = part[rep, 0:HEAD]
    for i in range(1, m):
        head = head + landed[i, 0:HEAD]
    mine[...] = head[0:9]
    grads[rep, me] = head[0:9]
    around, wide, across = [], [], {}
    for i in range(1, n):
        peer = lax.rem(me + i, n)
        around.append(send(mine, grads.at[rep, me], g_send.at[i], g_recv.at[i], "obs", peer))
    for j in range(1, m):
        peer = lax.rem(rep + j, m)
        across[j, 0] = send(mine, grads.at[rep, me], c_send.at[j, 0], c_recv.at[j, 0], "rep", peer)
    for copy in second:
        copy.wait_recv()
    rest = part[rep, ROWS - KEPT : ROWS]
    for i in range(1, m):
        rest = rest + landed[i, ROWS - KEPT : ROWS]
    total[...] = rest
    blocks[rep] = rest
    for j in range(1, m):
        peer = lax.rem(rep + j, m)
        wide.append(send(total, blocks.at[rep], b_send.at[j], b_recv.at[j], "rep", peer))
    for copy in first + second:
        copy.wait_send()
    lax.fori_loop(1, n, drain, 0)
    for i in range(1, n):
        around[i - 1].wait_recv()
        source = lax.rem(me - i + n, n)
        for j in range(1, m):
            peer = lax.rem(rep + j, m)
            piece = grads.at[rep, source]
            across[j, i] = send(piece, piece, c_send.at[j, i], c_recv.at[j, i], "rep", peer)
    for copy in wide:
        copy.wait()
    expand(blocks, out)

    def settle(i, carry):
        source = lax.rem(me - i + n, n)
        for j in range(1, m):
            piece = grads.at[rep, source]
            pltpu.make_async_remote_copy(
                src_ref=piece, dst_ref=piece, send_sem=c_send.at[j, i], recv_sem=c_recv.at[j, i],
                device_id={"rep": lax.rem(rep + j, m)}, device_id_type=MESH,
            ).wait_recv()
        place_chunk(source, grads, cmap, ready if early else None, spread)
        return carry

    lax.fori_loop(0, n, settle, 0, unroll=2)
    lay_out(spread, gradient)
    for copy in around:
        copy.wait_send()
    for copy in across.values():
        copy.wait_send()


def write_kernel(gradient, blocks, gradient_out, blocks_out, gradient_held, blocks_held, in_sem, out_sem):
    def cut(ref, count):
        step = ref.shape[1] // count
        return [ref.at[:, pl.ds(c * step, step)] for c in range(count)]

    jobs = list(zip(cut(blocks, 2), cut(blocks_held, 2), cut(blocks_out, 2)))
    jobs += list(zip(cut(gradient, 4), cut(gradient_held, 4), cut(gradient_out, 4)))
    reads = [pltpu.make_async_copy(job[0], job[1], in_sem.at[j]) for j, job in enumerate(jobs)]
    writes = [pltpu.make_async_copy(job[1], job[2], out_sem.at[j]) for j, job in enumerate(jobs)]
    for read in reads:
        read.start()
    for read, write in zip(reads, writes):
        read.wait()
        write.start()
    for write in writes:
        write.wait()


def local(jacobians, residuals, camera_local, bucket_counts, camera_map):
    n, m = lax.axis_size("obs"), lax.axis_size("rep")
    slots = jacobians.shape[1]
    cap = slots // n
    cams = camera_map.shape[0]
    width = CAM_DEV // m
    highs = cams // LOW
    dma = pltpu.SemaphoreType.DMA
    early = n if n * LOW * CAM_DEV * 2 <= 8 * 1024 * 1024 else 1
    limit = 60 * 1024 * 1024
    gradient, out = pl.pallas_call(
        functools.partial(main_kernel, n, m),
        out_shape=(jax.ShapeDtypeStruct((9, cams), F32), jax.ShapeDtypeStruct((81, CAM_DEV), F32)),
        in_specs=[pl.BlockSpec(memory_space=pltpu.SMEM)] + [pl.BlockSpec(memory_space=pltpu.HBM)] * 4,
        out_specs=(vspec(), vspec()),
        scratch_shapes=[
            VMEM((18, slots), F32),
            VMEM((2, slots), F32),
            VMEM((1, slots), jnp.int32),
            VMEM((1, cams), jnp.int32),
            dma((4,)),
            VMEM((m, KEPT, width), F32),
            VMEM((m, n, 9, width), F32),
            VMEM((early, LOW, CAM_DEV), BF16),
            VMEM((highs * 18, LOW), F32),
            VMEM((21, slots), F32),
            VMEM((n, 21, cap), F32),
            VMEM((ROWS, cap), F32),
            VMEM((m, ROWS, width), F32),
            VMEM((m, ROWS, width), F32),
            VMEM((KEPT, width), F32),
            VMEM((9, width), F32),
            dma((n,)),
            dma((n,)),
            dma((2, m)),
            dma((2, m)),
            dma((m,)),
            dma((m,)),
            dma((n,)),
            dma((n,)),
            dma((m, n)),
            dma((m, n)),
        ],
        compiler_params=pltpu.CompilerParams(collective_id=0, has_side_effects=True, vmem_limit_bytes=limit),
    )(bucket_counts, jacobians, residuals, camera_local.reshape(1, slots), camera_map.reshape(1, cams))
    anywhere = pl.BlockSpec(memory_space=pl.ANY)
    shapes = (jax.ShapeDtypeStruct(gradient.shape, F32), jax.ShapeDtypeStruct(out.shape, F32))
    return pl.pallas_call(
        write_kernel,
        out_shape=shapes,
        in_specs=[anywhere] * 2,
        out_specs=(anywhere, anywhere),
        scratch_shapes=[VMEM(gradient.shape, F32), VMEM(out.shape, F32), dma((6,)), dma((6,))],
        compiler_params=pltpu.CompilerParams(vmem_limit_bytes=limit),
    )(gradient, out)


def solution(mesh):
    in_specs = (
        P(None, ("obs", "rep")),
        P(None, ("obs", "rep")),
        P(("obs", "rep")),
        P(("obs", "rep"), None),
        P(),
    )
    out_specs = (P(), P(None, "obs"))
    return jax.shard_map(local, mesh=mesh, in_specs=in_specs, out_specs=out_specs, check_vma=False)
```

profile of v0, /device:TPU:1, one launch (start us, length us, event | category | flops | bytes accessed | tf_op | source)
XLA Modules:
  0.0 422.3 jit_solution(13005656109486539647)
XLA Ops:
  0.6 417.8 %shard_map.68 = (f32[9,65536]{1,0:T(8,128)}, f32[81,1024]{1,0:T(8,128)}) custom-call(s32[1,64]{1,0:T(1,128)} %counts.1, f32[18,32768]{1,0:T(8,128)} %jac_in.1, f32[2,32768]{1,0:T(2,128)} %res_in.1, s32[1,32768]{1,0:T(1,128)} %bitcast.3, s32[1,65536]{1,0:T(1,128)} %bitcast.2), custom_call_target="tpu_custom_call" | custom-call | tf_op jit(solution)/shard_map/pallas_call | solution.py:294
  418.4 3.9 shard_map.69
where the time goes:
time: 422 us
  Pallas kernels  422 us (100%)
    pallas_call x1, Pallas kernels, local(): pl.pallas_call(functools.partial(main_kernel, n, m), out_shape=(jax.Shape...  418 us

commit v1 on v0

v1 whole, which is shorter than its diff:
```python
import functools

import jax
import jax.numpy as jnp
from jax import lax
from jax.experimental import pallas as pl
from jax.experimental.pallas import tpu as pltpu
from jax.sharding import PartitionSpec as P

CAM_DEV = 1024
MESH = pl.DeviceIdType.MESH
F32 = jnp.float32
BF16 = jnp.bfloat16
VMEM = pltpu.VMEM
ROWS = 56
HEAD = 16
KEPT = 48
LOW = 256
LIVE = 256
NZ, NY, NX = 8, 4, 4
WINDOWS = (20, 34, 48)
DIMS = (((1,), (1,)), ((), ()))


def split(value):
    high = value.astype(BF16).astype(F32)
    return high, value - high


def one_hot_of(low, wide):
    shape = (wide, low.shape[1])
    rows = lax.broadcasted_iota(jnp.int32, shape, 0).astype(F32).astype(BF16)
    there = jnp.broadcast_to(low.astype(F32), shape).astype(BF16)
    return jnp.where(there == rows, jnp.ones(shape, BF16), jnp.zeros(shape, BF16))


def turn(value, j):
    return jnp.concatenate([value[j:8], value[0:j]], axis=0)


def block_row(k, l):
    k, l = min(k, l), max(k, l)
    if l == 8:
        return 12 if k == 8 else 48 + k
    j = l - k
    if j < 4:
        return 16 + 8 * j + k
    if j == 4:
        return 8 + k
    return 16 + 8 * (8 - j) + l


def add_block(block, acc):
    lead, trail = block[0:8], block[9:17]
    lead8, trail8, res0, res1 = block[8:9], block[17:18], block[18:19], block[19:20]
    ids = block[20:21].astype(jnp.int32)
    place = lax.broadcasted_iota(jnp.int32, lead.shape, 0)

    def mixed(rows, ninth, res):
        left = jnp.where(place < 4, rows, ninth)
        right = jnp.where(place < 4, turn(rows, 4), jnp.where(place == 4, ninth, res))
        return left * right

    groups = [lead * res0 + trail * res1, mixed(lead, lead8, res0) + mixed(trail, trail8, res1)]
    groups.append(lead * lead + trail * trail)
    for j in range(1, 4):
        groups.append(lead * turn(lead, j) + trail * turn(trail, j))
    groups.append(lead * lead8 + trail * trail8)
    high, low = split(jnp.concatenate(groups, axis=0))
    both = jnp.concatenate([high, low], axis=0).astype(BF16)
    pieces, _, width = acc.shape
    up = jnp.where(ids < 0, -1, ids // width)
    one_hot = one_hot_of(ids - up * width, width)
    up = jnp.broadcast_to(up.astype(F32), both.shape).astype(BF16)
    zero = jnp.zeros_like(both)
    lhs = jnp.concatenate([jnp.where(up == jnp.asarray(h, BF16), both, zero) for h in range(pieces)], axis=0)
    added = lax.dot_general(lhs, one_hot, DIMS, preferred_element_type=F32)
    for h in range(pieces):
        at = h * 2 * ROWS
        acc[h] += added[at : at + ROWS] + added[at + ROWS : at + 2 * ROWS]


def place_source(block, up, one_hot, acc):
    rows = jnp.concatenate([block[0:8], block[8:16]], axis=1)
    ninth = jnp.concatenate([block[16:17], block[17:18]], axis=1)
    high, low = split(rows)
    top = jnp.concatenate([high, low], axis=0).astype(BF16)
    high9, low9 = split(ninth)
    up16 = jnp.broadcast_to(up.astype(F32), top.shape).astype(BF16)
    none = jnp.zeros_like(top)
    tiles = [jnp.where(up16 == jnp.asarray(h, BF16), top, none) for h in range(16)]
    mask = up == lax.broadcasted_iota(jnp.int32, (16, up.shape[1]), 0)
    tiles.append(jnp.where(mask, high9, 0.0).astype(BF16))
    tiles.append(jnp.where(mask, low9, 0.0).astype(BF16))
    acc[...] += lax.dot_general(jnp.concatenate(tiles, axis=0), one_hot, DIMS, preferred_element_type=F32)


def main_kernel(
    n, m, counts, jac_in, res_in, ids_in, cmap_in, all_out, blocks_out,
    jac, res, ids, cmap, load_sem, packed, moved, part, landed, blocks, gath, ready, spread, shares, got, every,
    over, over_block, full, over_in, over_z, over_zin, over_m, over_yin, over_g,
    x_send, x_recv, a_send, a_recv, b_send, b_recv, g_send, g_recv, r_send, r_recv, z_send, z_recv, m_send, m_recv,
    l_send, l_recv, p_send, p_recv, ox_send, ox_recv, oz_send, oz_recv, oy_send, oy_recv, og_send, og_recv, out_sem, blocks_sem,
):
    me, rep = lax.axis_index("obs"), lax.axis_index("rep")
    z, y, c, x = me // (NY * 2), lax.rem(me // 2, NY), lax.rem(me, 2), rep
    p = jnp.where(c == 0, x, y)
    q = jnp.where(c == 0, y, x)
    cap = jac.shape[1] // n
    width = part.shape[2]

    def at(zz, yy, cc, xx):
        return {"obs": (zz * NY + yy) * 2 + cc, "rep": xx}

    def cross(pp, qq):
        return at(z, jnp.where(c == 0, qq, pp), c, jnp.where(c == 0, pp, qq))

    barrier = pltpu.get_barrier_semaphore()
    for i in range(1, n):
        pl.semaphore_signal(barrier, inc=1, device_id={"obs": lax.rem(me + i, n)}, device_id_type=MESH)
    for i in range(NY):
        for j in range(1, NX):
            peer = at(z, lax.rem(y + i, NY), c, lax.rem(x + j, NX))
            pl.semaphore_signal(barrier, inc=1, device_id=peer, device_id_type=MESH)
    chunks = load_sem.shape[0] - 3
    span = n // chunks
    loads = [pltpu.make_async_copy(s, d, load_sem.at[k]) for k, (s, d) in enumerate(((res_in, res), (ids_in, ids), (cmap_in, cmap)))]
    for k in range(chunks):
        lanes = pl.ds(k * span * cap, span * cap)
        loads.append(pltpu.make_async_copy(jac_in.at[:, lanes], jac.at[:, lanes], load_sem.at[3 + k]))
    for load in loads:
        load.start()
    part[...] = jnp.zeros_like(part)
    over[...] = jnp.zeros_like(over)
    spread[...] = jnp.zeros_like(spread)
    for load in loads[0:3]:
        load.wait()
    place = lax.broadcasted_iota(jnp.int32, (1, LIVE), 1)

    def pack(d, carry):
        lanes = pl.ds(pl.multiple_of(d * cap, cap), LIVE)
        rest = pl.ds(pl.multiple_of(d * cap + LIVE, LIVE), LIVE)
        packed[d, 0:18, :] = jac[:, lanes]
        packed[d, 18:20, :] = res[:, lanes]
        packed[d, 20:21, :] = jnp.where(place < counts[0, d], ids[:, lanes], -1).astype(F32)
        count = jnp.full((18, LIVE), counts[0, d], jnp.int32)
        late = jnp.where(place + LIVE < counts[0, d], ids[:, rest], -1).astype(F32)
        found = (jac[:, rest], res[:, rest], late, jnp.full((8, LIVE), d, jnp.int32))
        return tuple(jnp.where(count[0 : new.shape[0]] > LIVE, new, old) for new, old in zip(found, carry))

    kept = (jnp.zeros((18, LIVE), F32), jnp.zeros((2, LIVE), F32), jnp.full((1, LIVE), -1, F32), jnp.zeros((8, LIVE), jnp.int32))
    for k in range(chunks):
        loads[3 + k].wait()
        kept = lax.fori_loop(k * span, (k + 1) * span, pack, kept, unroll=4)
    over_block[0:18, :] = kept[0]
    over_block[18:20, :] = kept[1]
    over_block[20:21, :] = kept[2]
    full[...] = kept[3]
    add_block(over_block[...], over)
    pl.semaphore_wait(barrier, n - 1 + NY * (NX - 1))

    def remote(src, dst, s, r, peer):
        return pltpu.make_async_remote_copy(
            src_ref=src, dst_ref=dst, send_sem=s, recv_sem=r, device_id=peer, device_id_type=MESH
        )

    sent = []

    def send(*args):
        copy = remote(*args)
        copy.start()
        sent.append(copy)
        return copy

    def handing(i):
        peer = lax.rem(me + i, n)
        return remote(packed.at[peer], moved.at[i], x_send.at[i], x_recv.at[i], {"obs": peer})

    def start(i, carry):
        handing(i).start()
        return carry

    def take(i, carry):
        handing(i).wait_recv()
        add_block(moved[i], part)
        return carry

    def drain(i, carry):
        handing(i).wait_send()
        return carry

    over_x = []
    for i in (1, 3, 2):
        peer = lax.rem(rep + i, m)
        over_x.append(send(over.at[peer], over_in.at[i], ox_send.at[i], ox_recv.at[i], {"rep": peer}))
    lax.fori_loop(1, WINDOWS[0], start, 0)
    add_block(packed[me], part)

    def prepare(a, carry):
        owner = (a // 2 * NY + y) * 2 + lax.rem(a, 2)
        here = cmap[:, pl.ds(pl.multiple_of(owner * CAM_DEV + rep * width, width), width)]
        ready[a] = one_hot_of(lax.rem(here, LOW), LOW)
        return carry

    lax.fori_loop(0, 16, prepare, 0)
    for copy in over_x:
        copy.wait_recv()
    mine = over[rep] + over_in[1] + over_in[2] + over_in[3]
    for g in range(7):
        over_z[g] = mine[g * 8 : g * 8 + 8]
    over_z[7] = jnp.zeros_like(over_z[7])
    over_zs = []
    for i in range(1, NZ):
        zz = lax.rem(z + i, NZ)
        over_zs.append(send(over_z.at[zz], over_zin.at[i], oz_send.at[i], oz_recv.at[i], at(zz, y, c, x)))
    lax.fori_loop(WINDOWS[0], WINDOWS[1], start, 0)
    lax.fori_loop(1, 17, take, 0)
    for copy in over_zs:
        copy.wait_recv()
    mine = over_z[z]
    for i in range(1, NZ):
        mine = mine + over_zin[i]
    over_m[...] = mine
    over_ys = []
    e = y * 2 + c
    for i in range(1, 8):
        ee = lax.rem(e + i, 8)
        over_ys.append(send(over_m, over_yin.at[i], oy_send.at[i], oy_recv.at[i], at(z, ee // 2, lax.rem(ee, 2), x)))
    lax.fori_loop(WINDOWS[1], WINDOWS[2], start, 0)
    lax.fori_loop(17, 33, take, 0)
    for copy in over_ys:
        copy.wait_recv()
    mine = over_m[...]
    for i in range(1, 8):
        mine = mine + over_yin[i]
    over_g[z] = mine
    over_gs = []
    for i in range(1, NZ):
        over_gs.append(send(over_g.at[z], over_g.at[z], og_send.at[i], og_recv.at[i], at(lax.rem(z + i, NZ), y, c, x)))
    lax.fori_loop(WINDOWS[2], n, start, 0)
    lax.fori_loop(33, n, take, 0)

    first, second = [], []
    for half, rows, copies in ((0, pl.ds(0, HEAD), first), (1, pl.ds(HEAD, ROWS - HEAD), second)):
        for i in (1, 3, 2):
            peer = lax.rem(rep + i, m)
            copies.append(
                send(part.at[peer, rows], landed.at[i, rows], a_send.at[half, i], a_recv.at[half, i], {"rep": peer})
            )
    for i in range(1, NZ):
        slot = over_g.at[lax.rem(z + NZ - i, NZ)]
        remote(slot, slot, og_send.at[i], og_recv.at[i], at(lax.rem(z + i, NZ), y, c, x)).wait_recv()
    owned = full[...] == me
    for copy in first:
        copy.wait_recv()

    def total(g):
        rows = slice(g * 8, g * 8 + 8)
        value = part[rep, rows] + jnp.where(owned, over_g[g], 0.0)
        for i in range(1, m):
            value = value + landed[i, rows]
        return value

    top, mix = total(0), total(1)
    a_me = z * 2 + c
    gath[a_me, 0:8] = top[:, 0:128]
    gath[a_me, 8:16] = top[:, 128:256]
    gath[a_me, 16:17] = mix[5:6, 0:128]
    gath[a_me, 17:18] = mix[5:6, 128:256]
    for i in range(1, 16):
        aa = lax.rem(a_me + i, 16)
        send(gath.at[a_me], gath.at[a_me], g_send.at[i], g_recv.at[i], at(aa // 2, y, lax.rem(aa, 2), x))
    blocks[rep, 0:8] = mix
    for copy in second:
        copy.wait_recv()
    for g in range(2, 7):
        blocks[rep, g * 8 - 8 : g * 8] = total(g)
    wide = []
    for i in (1, 3, 2):
        peer = lax.rem(rep + i, m)
        wide.append(send(blocks.at[rep], blocks.at[rep], b_send.at[i], b_recv.at[i], {"rep": peer}))

    def settle(i, carry):
        a = lax.rem(a_me + 16 - i, 16)
        owner = (a // 2 * NY + y) * 2 + lax.rem(a, 2)
        here = cmap[:, pl.ds(pl.multiple_of(owner * CAM_DEV + rep * width, width), width)]
        place_source(gath[a], here // LOW - a_me * 16, ready[a], spread)
        return carry

    def arrive(i, carry):
        a = lax.rem(a_me + 16 - i, 16)
        aa = lax.rem(a_me + i, 16)
        remote(gath.at[a], gath.at[a], g_send.at[i], g_recv.at[i], at(aa // 2, y, lax.rem(aa, 2), x)).wait_recv()
        return settle(i, carry)

    settle(0, 0)
    lax.fori_loop(1, 16, arrive, 0)
    for u in range(16):
        value = spread[u * 16 : u * 16 + 8, :] + spread[u * 16 + 8 : u * 16 + 16, :]
        shares[u, 0:8] = value[:, 0:128]
        shares[u, 8:16] = value[:, 128:256]
        ninth = spread[256 + u : 257 + u, :] + spread[272 + u : 273 + u, :]
        shares[u, 16:17] = ninth[:, 0:128]
        shares[u, 17:18] = ninth[:, 128:256]
    s_me = p * 4 + q
    reduced = []
    for i in range(1, 16):
        ss = lax.rem(s_me + i, 16)
        reduced.append(send(shares.at[ss], got.at[i], r_send.at[i], r_recv.at[i], cross(ss // 4, lax.rem(ss, 4))))
    for copy in reduced:
        copy.wait_recv()
    value = shares[s_me]
    for i in range(1, 16):
        value = value + got[i]
    every[c, p, q, z] = value
    for i in (4, 3, 5, 2, 6, 1, 7):
        own = every.at[c, p, q, z]
        send(own, own, z_send.at[i], z_recv.at[i], at(lax.rem(z + i, NZ), y, c, x))
    for i in range(1, NZ):
        slot = every.at[c, p, q, lax.rem(z + NZ - i, NZ)]
        remote(slot, slot, z_send.at[i], z_recv.at[i], at(lax.rem(z + i, NZ), y, c, x)).wait_recv()
    outs = []

    def put(cc, pp, qq):
        copy = pltpu.make_async_copy(every.at[cc, pp, qq], all_out.at[cc, pp, qq], out_sem.at[cc, pp, qq])
        copy.start()
        outs.append(copy)

    other = at(z, y, 1 - c, x)

    def back(v, i):
        return lax.rem(v + 4 - i, 4)

    for i in (1, 3, 2):
        group = every.at[c, p, q]
        send(group, group, m_send.at[i], m_recv.at[i], cross(p, lax.rem(q + i, 4)))
    for i in (0, 1, 3, 2):
        group = every.at[c, p, back(q, i)]
        if i:
            remote(group, group, m_send.at[i], m_recv.at[i], cross(p, lax.rem(q + i, 4))).wait_recv()
        for j in (1, 3, 2):
            send(group, group, l_send.at[j, i], l_recv.at[j, i], cross(lax.rem(p + j, 4), q))
        send(group, group, p_send.at[0, i], p_recv.at[0, i], other)
        put(c, p, back(q, i))
    for i in (0, 1, 3, 2):
        for j in (1, 3, 2):
            group = every.at[c, back(p, j), back(q, i)]
            remote(group, group, l_send.at[j, i], l_recv.at[j, i], cross(lax.rem(p + j, 4), q)).wait_recv()
            send(group, group, p_send.at[j, i], p_recv.at[j, i], other)
            put(c, back(p, j), back(q, i))
    for copy in wide:
        copy.wait_recv()
    out_blocks = pltpu.make_async_copy(blocks, blocks_out, blocks_sem.at[0])
    out_blocks.start()
    for j in (0, 1, 3, 2):
        for i in (0, 1, 3, 2):
            group = every.at[1 - c, back(q, j), back(p, i)]
            remote(group, group, p_send.at[j, i], p_recv.at[j, i], other).wait_recv()
            put(1 - c, back(q, j), back(p, i))
    lax.fori_loop(1, n, drain, 0)
    for copy in sent:
        copy.wait_send()
    for copy in outs:
        copy.wait()
    out_blocks.wait()


def write_kernel(all_in, blocks_in, gradient_out, blocks_out, held, blocks, gradient, wide, in_sem, out_sem):
    reads = [pltpu.make_async_copy(all_in.at[:, :, :, k], held.at[:, :, :, k], in_sem.at[k]) for k in range(NZ)]
    reads.append(pltpu.make_async_copy(blocks_in, blocks, in_sem.at[NZ]))
    reads[NZ].start()
    for read in reads[:NZ]:
        read.start()
    step = gradient.shape[1] // NZ
    writes = []

    def write(src, dst, k):
        copy = pltpu.make_async_copy(src, dst, out_sem.at[k])
        copy.start()
        writes.append(copy)

    reads[NZ].wait()
    pieces, _, width = blocks.shape
    for k in range(9):
        for l in range(9):
            row = block_row(k, l) - 8
            for r in range(pieces):
                wide[k * 9 + l : k * 9 + l + 1, r * width : (r + 1) * width] = blocks[r, row : row + 1, :]
    write(wide, blocks_out, NZ)
    for k in range(NZ):
        reads[k].wait()
        for block in range(32):
            c, p, q = block // 16, block // 4 % 4, block % 4
            lanes = k * step + block * LOW
            value = held[c, p, q, k]
            gradient[0:8, lanes : lanes + 128] = value[0:8]
            gradient[0:8, lanes + 128 : lanes + 256] = value[8:16]
            gradient[8:9, lanes : lanes + 128] = value[16:17]
            gradient[8:9, lanes + 128 : lanes + 256] = value[17:18]
        lanes = pl.ds(k * step, step)
        write(gradient.at[:, lanes], gradient_out.at[:, lanes], k)
    for copy in writes:
        copy.wait()


def local(jacobians, residuals, camera_local, bucket_counts, camera_map):
    n, m = lax.axis_size("obs"), lax.axis_size("rep")
    slots = jacobians.shape[1]
    cams = camera_map.shape[0]
    width = CAM_DEV // m
    dma = pltpu.SemaphoreType.DMA
    limit = 60 * 1024 * 1024
    anywhere = pl.BlockSpec(memory_space=pl.ANY)
    hbm = pl.BlockSpec(memory_space=pltpu.HBM)
    gathered, blocks = pl.pallas_call(
        functools.partial(main_kernel, n, m),
        out_shape=(jax.ShapeDtypeStruct((2, 4, 4, NZ, 18, 128), F32), jax.ShapeDtypeStruct((m, KEPT, width), F32)),
        in_specs=[pl.BlockSpec(memory_space=pltpu.SMEM)] + [hbm] * 4,
        out_specs=(hbm, hbm),
        scratch_shapes=[
            VMEM((18, slots), F32),
            VMEM((2, slots), F32),
            VMEM((1, slots), jnp.int32),
            VMEM((1, cams), jnp.int32),
            dma((3 + 4,)),
            VMEM((n, 21, LIVE), F32),
            VMEM((n, 21, LIVE), F32),
            VMEM((m, ROWS, width), F32),
            VMEM((m, ROWS, width), F32),
            VMEM((m, KEPT, width), F32),
            VMEM((16, 18, 128), F32),
            VMEM((16, LOW, width), BF16),
            VMEM((288, LOW), F32),
            VMEM((16, 18, 128), F32),
            VMEM((16, 18, 128), F32),
            VMEM((2, 4, 4, NZ, 18, 128), F32),
            VMEM((m, ROWS, width), F32),
            VMEM((21, LIVE), F32),
            VMEM((8, LIVE), jnp.int32),
            VMEM((m, ROWS, width), F32),
            VMEM((NZ, 8, width), F32),
            VMEM((NZ, 8, width), F32),
            VMEM((8, width), F32),
            VMEM((8, 8, width), F32),
            VMEM((NZ, 8, width), F32),
        ]
        + [dma((n,))] * 2 + [dma((2, m))] * 2 + [dma((m,))] * 2 + [dma((16,))] * 4 + [dma((NZ,))] * 2 + [dma((4,))] * 2
        + [dma((4, 4))] * 4 + [dma((m,))] * 2 + [dma((NZ,))] * 2 + [dma((8,))] * 2 + [dma((NZ,))] * 2
        + [dma((2, 4, 4)), dma((1,))],
        compiler_params=pltpu.CompilerParams(collective_id=0, has_side_effects=True, vmem_limit_bytes=limit),
    )(bucket_counts, jacobians, residuals, camera_local.reshape(1, slots), camera_map.reshape(1, cams))
    shapes = (jax.ShapeDtypeStruct((9, cams), F32), jax.ShapeDtypeStruct((81, CAM_DEV), F32))
    return pl.pallas_call(
        write_kernel,
        out_shape=shapes,
        in_specs=[anywhere] * 2,
        out_specs=(anywhere, anywhere),
        scratch_shapes=[
            VMEM(gathered.shape, F32), VMEM(blocks.shape, F32), VMEM(shapes[0].shape, F32), VMEM(shapes[1].shape, F32),
            dma((NZ + 1,)), dma((NZ + 1,)),
        ],
        compiler_params=pltpu.CompilerParams(vmem_limit_bytes=limit),
    )(gathered, blocks)


def solution(mesh):
    in_specs = (
        P(None, ("obs", "rep")),
        P(None, ("obs", "rep")),
        P(("obs", "rep")),
        P(("obs", "rep"), None),
        P(),
    )
    out_specs = (P(), P(None, "obs"))
    return jax.shard_map(local, mesh=mesh, in_specs=in_specs, out_specs=out_specs, check_vma=False)
```

time: 422 us -> 111 us (0.26)
  Pallas kernels: 422 us -> 110 us
    pallas_call x1, Pallas kernels: 418 us -> 107 us  [local(): pl.pallas_call(functools.partial(main_kernel, n, m), out_shape=(jax.Shape...]
where the time goes in v1:
time: 111 us
  Pallas kernels  110 us (99%)
    pallas_call x1, Pallas kernels, local(): pl.pallas_call(functools.partial(main_kernel, n, m), out_shape=(jax.Shape...  107 us
    pallas_call x1, Pallas kernels, local(): pl.pallas_call(write_kernel, out_shape=shapes, in_specs=[anywhere] * 2, o...  3.34 us

profile of v1, /device:TPU:1, one launch (start us, length us, event | category | flops | bytes accessed | tf_op | source)
XLA Modules:
  0.0 110.7 jit_solution(4049248626665366433)
XLA Ops:
  0.6 106.7 %shard_map.68 = (f32[2,4,4,8,18,128]{5,4,3,2,1,0:T(8,128)}, f32[4,48,256]{2,1,0:T(8,128)}) custom-call(s32[1,64]{1,0:T(1,128)} %counts.1, f32[18,32768]{1,0:T(8,128)} %jac_in.1, f32[2,32768]{1,0:T(2,128)} %res_in.1, s32[1,32768]{1,0:T(1,128)} %bitcast.3, s32[1,65536]{1,0:T(1,128)} %bitcast.2), custom_call_target="tpu_custom_call" | custom-call | tf_op jit(solution)/shard_map/pallas_call | solution.py:415
  107.3 3.3 %shard_map.69 = (f32[9,65536]{1,0:T(8,128)}, f32[81,1024]{1,0:T(8,128)}) custom-call(f32[2,4,4,8,18,128]{5,4,3,2,1,0:T(8,128)} %get-tuple-element.4.all_in, f32[4,48,256]{2,1,0:T(8,128)} %get-tuple-element.5.blocks_in), custom_call_target="tpu_custom_call" | custom-call | tf_op jit(solution)/shard_map/pallas_call | solution.py:453

commit v2 on v1

v2 whole, which is shorter than its diff:
```python
import functools

import jax
import jax.numpy as jnp
from jax import lax
from jax.experimental import pallas as pl
from jax.experimental.pallas import tpu as pltpu
from jax.sharding import PartitionSpec as P

CAM_DEV = 1024
MESH = pl.DeviceIdType.MESH
F32 = jnp.float32
BF16 = jnp.bfloat16
VMEM = pltpu.VMEM
ROWS = 56
HEAD = 16
KEPT = 48
LOW = 256
LIVE = 256
NZ, NY, NX = 8, 4, 4
AGG = NX * NY * 2
DIMS = (((1,), (1,)), ((), ()))


def split(value):
    high = value.astype(BF16).astype(F32)
    return high, value - high


def one_hot_of(low, wide):
    shape = (wide, low.shape[1])
    rows = lax.broadcasted_iota(jnp.int32, shape, 0).astype(F32).astype(BF16)
    there = jnp.broadcast_to(low.astype(F32), shape).astype(BF16)
    return jnp.where(there == rows, jnp.ones(shape, BF16), jnp.zeros(shape, BF16))


def turn(value, j):
    return jnp.concatenate([value[j:8], value[0:j]], axis=0)


def block_row(k, l):
    k, l = min(k, l), max(k, l)
    if l == 8:
        return 12 if k == 8 else 48 + k
    j = l - k
    if j < 4:
        return 16 + 8 * j + k
    if j == 4:
        return 8 + k
    return 16 + 8 * (8 - j) + l


def add_block(block, acc):
    lead, trail = block[0:8], block[9:17]
    lead8, trail8, res0, res1 = block[8:9], block[17:18], block[18:19], block[19:20]
    ids = block[20:21].astype(jnp.int32)
    place = lax.broadcasted_iota(jnp.int32, lead.shape, 0)

    def mixed(rows, ninth, res):
        left = jnp.where(place < 4, rows, ninth)
        right = jnp.where(place < 4, turn(rows, 4), jnp.where(place == 4, ninth, res))
        return left * right

    groups = [lead * res0 + trail * res1, mixed(lead, lead8, res0) + mixed(trail, trail8, res1)]
    groups.append(lead * lead + trail * trail)
    for j in range(1, 4):
        groups.append(lead * turn(lead, j) + trail * turn(trail, j))
    groups.append(lead * lead8 + trail * trail8)
    high, low = split(jnp.concatenate(groups, axis=0))
    both = jnp.concatenate([high, low], axis=0).astype(BF16)
    pieces, _, width = acc.shape
    up = jnp.where(ids < 0, -1, ids // width)
    one_hot = one_hot_of(ids - up * width, width)
    up = jnp.broadcast_to(up.astype(F32), both.shape).astype(BF16)
    zero = jnp.zeros_like(both)
    lhs = jnp.concatenate([jnp.where(up == jnp.asarray(h, BF16), both, zero) for h in range(pieces)], axis=0)
    added = lax.dot_general(lhs, one_hot, DIMS, preferred_element_type=F32)
    for h in range(pieces):
        at = h * 2 * ROWS
        acc[h, 0:ROWS] += added[at : at + ROWS] + added[at + ROWS : at + 2 * ROWS]


def place_source(block, up, one_hot, acc):
    rows = jnp.concatenate([block[0:8], block[8:16]], axis=1)
    ninth = jnp.concatenate([block[16:17], block[17:18]], axis=1)
    high, low = split(rows)
    top = jnp.concatenate([high, low], axis=0).astype(BF16)
    high9, low9 = split(ninth)
    up16 = jnp.broadcast_to(up.astype(F32), top.shape).astype(BF16)
    none = jnp.zeros_like(top)
    tiles = [jnp.where(up16 == jnp.asarray(h, BF16), top, none) for h in range(16)]
    mask = up == lax.broadcasted_iota(jnp.int32, (16, up.shape[1]), 0)
    tiles.append(jnp.where(mask, high9, 0.0).astype(BF16))
    tiles.append(jnp.where(mask, low9, 0.0).astype(BF16))
    acc[...] += lax.dot_general(jnp.concatenate(tiles, axis=0), one_hot, DIMS, preferred_element_type=F32)


def main_kernel(
    n, m, counts, jac_in, res_in, ids_in, cmap_in, all_out, nine_out, blocks_out,
    jac, res, ids, cmap, load_sem, packed, moved, part, landed, owned_blocks, blocks, gath, ready, spread, shares, got,
    every, nine, over, over_block, full, over_zin, over_m, over_xin, over_n, over_yin, over_g,
    x_send, x_recv, a_send, a_recv, b_send, b_recv, g_send, g_recv, r_send, r_recv, z_send, z_recv, m_send, m_recv,
    l_send, l_recv, p_send, p_recv, oz_send, oz_recv, ox_send, ox_recv, oy_send, oy_recv, og_send, og_recv, out_sem, blocks_sem,
):
    me, rep = lax.axis_index("obs"), lax.axis_index("rep")
    z, y, c, x = me // (NY * 2), lax.rem(me // 2, NY), lax.rem(me, 2), rep
    p = jnp.where(c == 0, x, y)
    q = jnp.where(c == 0, y, x)
    cap = jac.shape[1] // n
    width = part.shape[2]
    e = (x * NY + y) * 2 + c
    half, quarter = z // 4, lax.rem(z, 4)

    def at(zz, yy, cc, xx):
        return {"obs": (zz * NY + yy) * 2 + cc, "rep": xx}

    def cross(pp, qq):
        return at(z, jnp.where(c == 0, qq, pp), c, jnp.where(c == 0, pp, qq))

    chunks = load_sem.shape[0] - 3
    span = n // chunks
    loads = [pltpu.make_async_copy(s, d, load_sem.at[k]) for k, (s, d) in enumerate(((res_in, res), (ids_in, ids), (cmap_in, cmap)))]
    for k in range(chunks):
        lanes = pl.ds(k * span * cap, span * cap)
        loads.append(pltpu.make_async_copy(jac_in.at[:, lanes], jac.at[:, lanes], load_sem.at[3 + k]))
    for load in loads:
        load.start()
    barrier = pltpu.get_barrier_semaphore()

    def plane(i):
        ee = lax.rem(e + i, AGG)
        return at(z, lax.rem(ee // 2, NY), lax.rem(ee, 2), ee // (NY * 2))

    peers = [plane(i) for i in range(1, AGG)]
    for i in range(1, NZ):
        zz = lax.rem(z + i, NZ)
        peers.append(at(zz, y, 1 - c, x))
        for j in range(NX):
            peers.append(at(zz, y, c, lax.rem(x + j, NX)))
    for peer in peers:
        pl.semaphore_signal(barrier, inc=1, device_id=peer, device_id_type=MESH)
    part[...] = jnp.zeros_like(part)
    over[...] = jnp.zeros_like(over)
    spread[...] = jnp.zeros_like(spread)
    for load in loads:
        load.wait()
    place = lax.broadcasted_iota(jnp.int32, (1, LIVE), 1)

    def pack(ee, b):
        d = (ee // 8 * 2 + b) * 8 + lax.rem(ee, 8)
        lanes = pl.ds(pl.multiple_of(d * cap, cap), LIVE)
        packed[ee, b, 0:18, :] = jac[:, lanes]
        packed[ee, b, 18:20, :] = res[:, lanes]
        packed[ee, b, 20:21, :] = jnp.where(place < counts[0, d], ids[:, lanes], -1).astype(F32)

    def scan(d, carry):
        rest = pl.ds(pl.multiple_of(d * cap + LIVE, LIVE), LIVE)
        count = jnp.full((18, LIVE), counts[0, d], jnp.int32)
        late = jnp.where(place + LIVE < counts[0, d], ids[:, rest], -1).astype(F32)
        found = (jac[:, rest], res[:, rest], late, jnp.full((8, LIVE), d, jnp.int32))
        return tuple(jnp.where(count[0 : new.shape[0]] > LIVE, new, old) for new, old in zip(found, carry))

    pl.semaphore_wait(barrier, len(peers))

    def remote(src, dst, s, r, peer):
        return pltpu.make_async_remote_copy(
            src_ref=src, dst_ref=dst, send_sem=s, recv_sem=r, device_id=peer, device_id_type=MESH
        )

    sent = []

    def send(*args):
        copy = remote(*args)
        copy.start()
        sent.append(copy)
        return copy

    def handing(k):
        i = AGG // 2 + (k + 1) // 2 * (1 - 2 * lax.rem(k, 2))
        return remote(packed.at[lax.rem(e + i, AGG)], moved.at[i], x_send.at[i], x_recv.at[i], plane(i))

    def start(k, carry):
        i = AGG // 2 + (k + 1) // 2 * (1 - 2 * lax.rem(k, 2))
        ee = lax.rem(e + i, AGG)
        pack(ee, 0)
        pack(ee, 1)
        handing(k).start()
        return carry

    def take(k, carry):
        i = AGG // 2 + (k + 1) // 2 * (1 - 2 * lax.rem(k, 2))
        handing(k).wait_recv()
        add_block(moved[i, 0], part.at[0:4])
        add_block(moved[i, 1], part.at[4:8])
        return carry

    def drain(k, carry):
        handing(k).wait_send()
        return carry

    far = (4, 3, 5, 2, 6, 1, 7)
    lax.fori_loop(0, 6, start, 0)
    kept = (jnp.zeros((18, LIVE), F32), jnp.zeros((2, LIVE), F32), jnp.full((1, LIVE), -1, F32), jnp.zeros((8, LIVE), jnp.int32))
    kept = lax.fori_loop(0, n, scan, kept, unroll=4)
    over_block[0:18, :] = kept[0]
    over_block[18:20, :] = kept[1]
    over_block[20:21, :] = kept[2]
    full[...] = kept[3]
    add_block(over_block[...], over)

    def over_part(zz):
        return over.at[lax.rem(zz, 4), pl.ds(pl.multiple_of(zz // 4 * 32, 32), 32)]

    over_zs = []
    for i in far:
        zz = lax.rem(z + i, NZ)
        over_zs.append(send(over_part(zz), over_zin.at[i], oz_send.at[i], oz_recv.at[i], at(zz, y, c, x)))
    lax.fori_loop(6, 14, start, 0)
    pack(e, 0)
    pack(e, 1)
    add_block(packed[e, 0], part.at[0:4])
    add_block(packed[e, 1], part.at[4:8])

    def owner_lanes(a):
        owner = (a // NY * 2 + half) * 8 + lax.rem(a, NY) * 2 + c
        return pl.ds(pl.multiple_of(owner * CAM_DEV + quarter * width, width), width)

    def prepare(a, carry):
        ready[a] = one_hot_of(lax.rem(cmap[:, owner_lanes(a)], LOW), LOW)
        return carry

    lax.fori_loop(0, 16, prepare, 0)
    lax.fori_loop(0, 8, take, 0)
    lax.fori_loop(14, 20, start, 0)
    lax.fori_loop(8, 14, take, 0)
    for copy in over_zs:
        copy.wait_recv()
    mine = over_part(z)[...]
    for i in range(1, NZ):
        mine = mine + over_zin[i]
    over_m[...] = mine
    over_xs = []
    for i in (1, 3, 2):
        over_xs.append(send(over_m, over_xin.at[i], ox_send.at[i], ox_recv.at[i], at(z, y, c, lax.rem(x + i, NX))))
    lax.fori_loop(20, 26, start, 0)
    lax.fori_loop(14, 20, take, 0)
    for copy in over_xs:
        copy.wait_recv()
    over_n[...] = over_m[...] + over_xin[1] + over_xin[2] + over_xin[3]
    over_ys = []
    f = y * 2 + c
    for i in (4, 3, 5, 2, 6, 1, 7):
        ff = lax.rem(f + i, 8)
        over_ys.append(send(over_n, over_yin.at[i], oy_send.at[i], oy_recv.at[i], at(z, ff // 2, lax.rem(ff, 2), x)))
    lax.fori_loop(26, AGG - 1, start, 0)
    lax.fori_loop(20, AGG - 1, take, 0)
    first, second = [], []
    for kind, rows, copies in ((0, pl.ds(0, HEAD), first), (1, pl.ds(HEAD, ROWS - HEAD), second)):
        if kind:
            for copy in over_ys:
                copy.wait_recv()
            mine = over_n[...]
            for i in range(1, 8):
                mine = mine + over_yin[i]
            over_g[half] = mine
            send(over_g.at[half], over_g.at[half], og_send.at[0], og_recv.at[0], at(lax.rem(z + 4, NZ), y, c, x))
        for i in far:
            zz = lax.rem(z + i, NZ)
            copies.append(
                send(part.at[zz, rows], landed.at[i, rows], a_send.at[kind, i], a_recv.at[kind, i], at(zz, y, c, x))
            )
    other_half = over_g.at[1 - half]
    remote(other_half, other_half, og_send.at[0], og_recv.at[0], at(lax.rem(z + 4, NZ), y, c, x)).wait_recv()
    bucket = (x * 2 + half) * 8 + y * 2 + c
    owned = full[...] == bucket
    for copy in first:
        copy.wait_recv()

    def total(g):
        rows = slice(g * 8, g * 8 + 8)
        value = part[z, rows] + jnp.where(owned, over_g[g // 4, g % 4 * 8 : g % 4 * 8 + 8], 0.0)
        for i in range(1, NZ):
            value = value + landed[i, rows]
        return value

    top, mix = total(0), total(1)
    a_me = x * NY + y
    gath[a_me, 0:8] = top[:, 0:128]
    gath[a_me, 8:16] = top[:, 128:256]
    gath[a_me, 16:17] = mix[5:6, 0:128]
    gath[a_me, 17:18] = mix[5:6, 128:256]
    def gathering(i):
        a, aa = lax.rem(a_me + 16 - i, 16), lax.rem(a_me + i, 16)
        return gath.at[a], at(z, lax.rem(aa, NY), c, aa // NY)

    for i in (8, 7, 9, 6, 10, 5, 11, 4, 12, 3, 13, 2, 14, 1, 15):
        send(gath.at[a_me], gath.at[a_me], g_send.at[i], g_recv.at[i], gathering(i)[1])
    owned_blocks[0:8] = mix
    for copy in second:
        copy.wait_recv()
    for g in range(2, 7):
        owned_blocks[g * 8 - 8 : g * 8] = total(g)
    home = x * 2 + half
    for j in range(1, NX):
        peer = at(home, y, c, lax.rem(x + j, NX))
        send(owned_blocks, blocks.at[quarter], b_send.at[j], b_recv.at[quarter], peer)

    def to_home():
        return remote(owned_blocks, blocks.at[quarter], b_send.at[0], b_recv.at[quarter], at(home, y, c, x))

    @pl.when(home != z)
    def _():
        to_home().start()

    @pl.when(home == z)
    def _():
        blocks[quarter] = owned_blocks[...]

    def settle(i, carry):
        a = lax.rem(a_me + 16 - i, 16)
        place_source(gath[a], cmap[:, owner_lanes(a)] // LOW - a_me * 16, ready[a], spread)
        return carry

    def arrive(i, carry):
        slot, peer = gathering(i)
        remote(slot, slot, g_send.at[i], g_recv.at[i], peer).wait_recv()
        return settle(i, carry)

    settle(0, 0)
    lax.fori_loop(1, 16, arrive, 0)
    for u in range(16):
        value = spread[u * 16 : u * 16 + 8, :] + spread[u * 16 + 8 : u * 16 + 16, :]
        shares[u, 0:8] = value[:, 0:128]
        shares[u, 8:16] = value[:, 128:256]
        ninth = spread[256 + u : 257 + u, :] + spread[272 + u : 273 + u, :]
        shares[u, 16:17] = ninth[:, 0:128]
        shares[u, 17:18] = ninth[:, 128:256]
    s_me = z * 2 + c
    reduced = []
    for i in (8, 7, 9, 6, 10, 5, 11, 4, 12, 3, 13, 2, 14, 1, 15):
        ss = lax.rem(s_me + i, 16)
        reduced.append(send(shares.at[ss], got.at[i], r_send.at[i], r_recv.at[i], at(ss // 2, y, lax.rem(ss, 2), x)))
    for copy in reduced:
        copy.wait_recv()
    value = shares[s_me]
    for i in range(1, 16):
        value = value + got[i]
    every[c, p, q, z] = value[0:16]
    nine[c, p, q, z] = value[16:18]
    held = (every, nine)
    for i in far:
        for v in (0, 1):
            own = held[v].at[c, p, q, z]
            send(own, own, z_send.at[v, i], z_recv.at[v, i], at(lax.rem(z + i, NZ), y, c, x))
    for i in range(1, NZ):
        for v in (0, 1):
            slot = held[v].at[c, p, q, lax.rem(z + NZ - i, NZ)]
            remote(slot, slot, z_send.at[v, i], z_recv.at[v, i], at(lax.rem(z + i, NZ), y, c, x)).wait_recv()
    outs = []

    def put(v, cc, pp, qq):
        target = (all_out, nine_out)[v]
        copy = pltpu.make_async_copy(held[v].at[cc, pp, qq], target.at[cc, pp, qq], out_sem.at[v, cc, pp, qq])
        copy.start()
        outs.append(copy)

    other = at(z, y, 1 - c, x)

    def back(v, i):
        return lax.rem(v + 4 - i, 4)

    for i in (1, 3, 2):
        for v in (0, 1):
            group = held[v].at[c, p, q]
            send(group, group, m_send.at[v, i], m_recv.at[v, i], cross(p, lax.rem(q + i, 4)))
    for i in (0, 1, 3, 2):
        for v in (0, 1):
            group = held[v].at[c, p, back(q, i)]
            if i:
                remote(group, group, m_send.at[v, i], m_recv.at[v, i], cross(p, lax.rem(q + i, 4))).wait_recv()
            for j in (1, 3, 2):
                send(group, group, l_send.at[v, j, i], l_recv.at[v, j, i], cross(lax.rem(p + j, 4), q))
            send(group, group, p_send.at[v, 0, i], p_recv.at[v, 0, i], other)
            put(v, c, p, back(q, i))
    for i in (0, 1, 3, 2):
        for j in (1, 3, 2):
            for v in (0, 1):
                group = held[v].at[c, back(p, j), back(q, i)]
                remote(group, group, l_send.at[v, j, i], l_recv.at[v, j, i], cross(lax.rem(p + j, 4), q)).wait_recv()
                send(group, group, p_send.at[v, j, i], p_recv.at[v, j, i], other)
                put(v, c, back(p, j), back(q, i))
    for k in range(4):
        slot = blocks.at[k]
        source = lax.rem(z, 2) * 4 + k
        mine_here = (x == z // 2) & (source == z)

        @pl.when(jnp.logical_not(mine_here))
        def _():
            remote(slot, slot, b_send.at[0], b_recv.at[k], at(home, y, c, lax.rem(x + 1, NX))).wait_recv()

    @pl.when(home != z)
    def _():
        to_home().wait_send()

    out_blocks = pltpu.make_async_copy(blocks, blocks_out, blocks_sem.at[0])
    out_blocks.start()
    for j in (0, 1, 3, 2):
        for i in (0, 1, 3, 2):
            for v in (0, 1):
                group = held[v].at[1 - c, back(q, j), back(p, i)]
                remote(group, group, p_send.at[v, j, i], p_recv.at[v, j, i], other).wait_recv()
                put(v, 1 - c, back(q, j), back(p, i))
    lax.fori_loop(0, AGG - 1, drain, 0)
    for copy in sent:
        copy.wait_send()
    for copy in outs:
        copy.wait()
    out_blocks.wait()


def write_kernel(all_in, nine_in, blocks_in, gradient_out, blocks_out, held, nine, blocks, gradient, wide, in_sem, out_sem):
    reads = []
    for k in range(NX * NY):
        x, y = k // NY, k % NY
        for v, (src, dst) in enumerate(((all_in, held), (nine_in, nine))):
            for c, (p, q) in enumerate(((x, y), (y, x))):
                reads.append(pltpu.make_async_copy(src.at[c, p, q], dst.at[c, p, q], in_sem.at[k * 4 + v * 2 + c]))
    last = NX * NY
    reads.append(pltpu.make_async_copy(blocks_in, blocks, in_sem.at[last * 4]))
    for read in reads:
        read.start()
    step = gradient.shape[1] // last
    writes = []

    def write(src, dst, k):
        copy = pltpu.make_async_copy(src, dst, out_sem.at[k])
        copy.start()
        writes.append(copy)

    reads[last * 4].wait()
    pieces, _, width = blocks.shape
    for k in range(9):
        for l in range(9):
            row = block_row(k, l) - 8
            for r in range(pieces):
                wide[k * 9 + l : k * 9 + l + 1, r * width : (r + 1) * width] = blocks[r, row : row + 1, :]
    write(wide, blocks_out, last)
    for k in range(last):
        for read in reads[k * 4 : k * 4 + 4]:
            read.wait()
        x, y = k // NY, k % NY
        for block in range(16):
            z, c = block // 2, block % 2
            p, q = (y, x) if c else (x, y)
            lanes = k * step + block * LOW
            gradient[0:8, lanes : lanes + 128] = held[c, p, q, z, 0:8]
            gradient[0:8, lanes + 128 : lanes + 256] = held[c, p, q, z, 8:16]
            gradient[8:9, lanes : lanes + 128] = nine[c, p, q, z, 0:1]
            gradient[8:9, lanes + 128 : lanes + 256] = nine[c, p, q, z, 1:2]
        lanes = pl.ds(k * step, step)
        write(gradient.at[:, lanes], gradient_out.at[:, lanes], k)
    for copy in writes:
        copy.wait()


def local(jacobians, residuals, camera_local, bucket_counts, camera_map):
    n, m = lax.axis_size("obs"), lax.axis_size("rep")
    slots = jacobians.shape[1]
    cams = camera_map.shape[0]
    width = CAM_DEV // m
    dma = pltpu.SemaphoreType.DMA
    limit = 60 * 1024 * 1024
    anywhere = pl.BlockSpec(memory_space=pl.ANY)
    hbm = pl.BlockSpec(memory_space=pltpu.HBM)
    gathered, ninth, blocks = pl.pallas_call(
        functools.partial(main_kernel, n, m),
        out_shape=(
            jax.ShapeDtypeStruct((2, 4, 4, NZ, 16, 128), F32),
            jax.ShapeDtypeStruct((2, 4, 4, NZ, 2, 128), F32),
            jax.ShapeDtypeStruct((m, KEPT, width), F32),
        ),
        in_specs=[pl.BlockSpec(memory_space=pltpu.SMEM)] + [hbm] * 4,
        out_specs=(hbm, hbm, hbm),
        scratch_shapes=[
            VMEM((18, slots), F32),
            VMEM((2, slots), F32),
            VMEM((1, slots), jnp.int32),
            VMEM((1, cams), jnp.int32),
            dma((3 + 4,)),
            VMEM((AGG, 2, 21, LIVE), F32),
            VMEM((AGG, 2, 21, LIVE), F32),
            VMEM((NZ, ROWS, width), F32),
            VMEM((NZ, ROWS, width), F32),
            VMEM((KEPT, width), F32),
            VMEM((m, KEPT, width), F32),
            VMEM((16, 18, 128), F32),
            VMEM((16, LOW, width), BF16),
            VMEM((288, LOW), F32),
            VMEM((16, 18, 128), F32),
            VMEM((16, 18, 128), F32),
            VMEM((2, 4, 4, NZ, 16, 128), F32),
            VMEM((2, 4, 4, NZ, 2, 128), F32),
            VMEM((m, 64, width), F32),
            VMEM((21, LIVE), F32),
            VMEM((8, LIVE), jnp.int32),
            VMEM((NZ, 32, width), F32),
            VMEM((32, width), F32),
            VMEM((NX, 32, width), F32),
            VMEM((32, width), F32),
            VMEM((8, 32, width), F32),
            VMEM((2, 32, width), F32),
        ]
        + [dma((AGG,))] * 2 + [dma((2, NZ))] * 2 + [dma((4,))] * 2 + [dma((16,))] * 4 + [dma((2, NZ))] * 2 + [dma((2, 4))] * 2
        + [dma((2, 4, 4))] * 4 + [dma((NZ,))] * 2 + [dma((NX,))] * 2 + [dma((8,))] * 2 + [dma((1,))] * 2
        + [dma((2, 2, 4, 4)), dma((1,))],
        compiler_params=pltpu.CompilerParams(collective_id=0, has_side_effects=True, vmem_limit_bytes=limit),
    )(bucket_counts, jacobians, residuals, camera_local.reshape(1, slots), camera_map.reshape(1, cams))
    shapes = (jax.ShapeDtypeStruct((9, cams), F32), jax.ShapeDtypeStruct((81, CAM_DEV), F32))
    return pl.pallas_call(
        write_kernel,
        out_shape=shapes,
        in_specs=[anywhere] * 3,
        out_specs=(anywhere, anywhere),
        scratch_shapes=[
            VMEM(gathered.shape, F32), VMEM(ninth.shape, F32), VMEM(blocks.shape, F32), VMEM(shapes[0].shape, F32),
            VMEM(shapes[1].shape, F32), dma((NX * NY * 4 + 1,)), dma((NX * NY + 1,)),
        ],
        compiler_params=pltpu.CompilerParams(vmem_limit_bytes=limit),
    )(gathered, ninth, blocks)


def solution(mesh):
    in_specs = (
        P(None, ("obs", "rep")),
        P(None, ("obs", "rep")),
        P(("obs", "rep")),
        P(("obs", "rep"), None),
        P(),
    )
    out_specs = (P(), P(None, "obs"))
    return jax.shard_map(local, mesh=mesh, in_specs=in_specs, out_specs=out_specs, check_vma=False)
```

time: 111 us -> 110 us (level)
  Pallas kernels: 110 us -> 108 us
    pallas_call x1, Pallas kernels: 107 us -> 104 us  [local(): pl.pallas_call(functools.partial(main_kernel, n, m), out_shape=(jax.Shape...]
    pallas_call x1, Pallas kernels: 3.34 us -> 4.82 us  [local(): pl.pallas_call(write_kernel, out_shape=shapes, in_specs=[anywhere] * 3, o...]
where the time goes in v2:
time: 110 us; the launch traced here: 109 us
  Pallas kernels  108 us (98%)
    pallas_call x1, Pallas kernels, local(): pl.pallas_call(functools.partial(main_kernel, n, m), out_shape=(jax.Shape...  104 us
    pallas_call x1, Pallas kernels, local(): pl.pallas_call(write_kernel, out_shape=shapes, in_specs=[anywhere] * 3, o...  4.82 us

profile of v2, /device:TPU:1, one launch (start us, length us, event | category | flops | bytes accessed | tf_op | source)
XLA Modules:
  0.0 109.1 jit_solution(5067994763963941433)
XLA Ops:
  0.6 103.6 %shard_map.68 = (f32[2,4,4,8,16,128]{5,4,3,2,1,0:T(8,128)}, f32[2,4,4,8,2,128]{5,4,3,2,1,0:T(2,128)}, f32[4,48,256]{2,1,0:T(8,128)}) custom-call(s32[1,64]{1,0:T(1,128)} %counts.1, f32[18,32768]{1,0:T(8,128)} %jac_in.1, f32[2,32768]{1,0:T(2,128)} %res_in.1, s32[1,32768]{1,0:T(1,128)} %bitcast.3, s32[1,65536]{1,0:T(1,128)} %bitcast.2), custom_call_target="tpu_custom_call" | custom-call | tf_op jit(solution)/shard_map/pallas_call | solution.py:475
  104.3 4.8 %shard_map.69 = (f32[9,65536]{1,0:T(8,128)}, f32[81,1024]{1,0:T(8,128)}) custom-call(f32[2,4,4,8,16,128]{5,4,3,2,1,0:T(8,128)} %get-tuple-element.5.all_in, f32[2,4,4,8,2,128]{5,4,3,2,1,0:T(2,128)} %get-tuple-element.6.nine_in, f32[4,48,256]{2,1,0:T(8,128)} %get-tuple-element.7.blocks_in), custom_call_target="tpu_custom_call" | custom-call | tf_op jit(solution)/shard_map/pallas_call | solution.py:519

commit v3 on v2

--- a/solution.py
+++ b/solution.py
@@ -97,10 +97,10 @@
 
 def main_kernel(
     n, m, counts, jac_in, res_in, ids_in, cmap_in, all_out, nine_out, blocks_out,
-    jac, res, ids, cmap, load_sem, packed, moved, part, landed, owned_blocks, blocks, gath, ready, spread, shares, got,
-    every, nine, over, over_block, full, over_zin, over_m, over_xin, over_n, over_yin, over_g,
-    x_send, x_recv, a_send, a_recv, b_send, b_recv, g_send, g_recv, r_send, r_recv, z_send, z_recv, m_send, m_recv,
-    l_send, l_recv, p_send, p_recv, oz_send, oz_recv, ox_send, ox_recv, oy_send, oy_recv, og_send, og_recv, out_sem, blocks_sem,
+    jac, res, ids, cmap, load_sem, packed, moved, part, landed, row_blocks, blocks, gath, ready, spread, shares, got,
+    every, nine, over, over_block, full, over_zin, over_s, over_in, over_all,
+    x_send, x_recv, a_send, a_recv, b_send, b_recv, h_send, h_recv, g_send, g_recv, r_send, r_recv, z_send, z_recv,
+    m_send, m_recv, l_send, l_recv, p_send, p_recv, oz_send, oz_recv, or_send, or_recv, og_send, og_recv, out_sem, blocks_sem,
 ):
     me, rep = lax.axis_index("obs"), lax.axis_index("rep")
     z, y, c, x = me // (NY * 2), lax.rem(me // 2, NY), lax.rem(me, 2), rep
@@ -134,9 +134,8 @@
     peers = [plane(i) for i in range(1, AGG)]
     for i in range(1, NZ):
         zz = lax.rem(z + i, NZ)
+        peers.append(at(zz, y, c, x))
         peers.append(at(zz, y, 1 - c, x))
-        for j in range(NX):
-            peers.append(at(zz, y, c, lax.rem(x + j, NX)))
     for peer in peers:
         pl.semaphore_signal(barrier, inc=1, device_id=peer, device_id_type=MESH)
     part[...] = jnp.zeros_like(part)
@@ -208,14 +207,11 @@
     full[...] = kept[3]
     add_block(over_block[...], over)
 
-    def over_part(zz):
-        return over.at[lax.rem(zz, 4), pl.ds(pl.multiple_of(zz // 4 * 32, 32), 32)]
-
     over_zs = []
     for i in far:
         zz = lax.rem(z + i, NZ)
-        over_zs.append(send(over_part(zz), over_zin.at[i], oz_send.at[i], oz_recv.at[i], at(zz, y, c, x)))
-    lax.fori_loop(6, 14, start, 0)
+        over_zs.append(send(over.at[lax.rem(zz, 4)], over_zin.at[i], oz_send.at[i], oz_recv.at[i], at(zz, y, c, x)))
+    lax.fori_loop(6, AGG - 1, start, 0)
     pack(e, 0)
     pack(e, 1)
     add_block(packed[e, 0], part.at[0:4])
@@ -230,47 +226,55 @@
         return carry
 
     lax.fori_loop(0, 16, prepare, 0)
-    lax.fori_loop(0, 8, take, 0)
-    lax.fori_loop(14, 20, start, 0)
-    lax.fori_loop(8, 14, take, 0)
+    lax.fori_loop(0, 24, take, 0)
     for copy in over_zs:
         copy.wait_recv()
-    mine = over_part(z)[...]
+    mine = over[quarter]
     for i in range(1, NZ):
         mine = mine + over_zin[i]
-    over_m[...] = mine
-    over_xs = []
-    for i in (1, 3, 2):
-        over_xs.append(send(over_m, over_xin.at[i], ox_send.at[i], ox_recv.at[i], at(z, y, c, lax.rem(x + i, NX))))
-    lax.fori_loop(20, 26, start, 0)
-    lax.fori_loop(14, 20, take, 0)
-    for copy in over_xs:
-        copy.wait_recv()
-    over_n[...] = over_m[...] + over_xin[1] + over_xin[2] + over_xin[3]
-    over_ys = []
-    f = y * 2 + c
-    for i in (4, 3, 5, 2, 6, 1, 7):
-        ff = lax.rem(f + i, 8)
-        over_ys.append(send(over_n, over_yin.at[i], oy_send.at[i], oy_recv.at[i], at(z, ff // 2, lax.rem(ff, 2), x)))
-    lax.fori_loop(26, AGG - 1, start, 0)
-    lax.fori_loop(20, AGG - 1, take, 0)
+    for k in range(ROWS // 2):
+        over_s[k] = mine[k * 2 : k * 2 + 2]
+    for k in range(ROWS // 2, AGG):
+        over_s[k] = jnp.zeros_like(over_s[k])
+
+    def scattering(i, carry):
+        remote(over_s.at[lax.rem(e + i, AGG)], over_in.at[i], or_send.at[i], or_recv.at[i], plane(i)).start()
+        return carry
+
+    def gathering_over(i):
+        slot = over_all.at[lax.rem(e + AGG - i, AGG)]
+        return remote(slot, slot, og_send.at[i], og_recv.at[i], plane(i))
+
+    def spreading(i, carry):
+        slot = over_all.at[e]
+        remote(slot, slot, og_send.at[i], og_recv.at[i], plane(i)).start()
+        return carry
+
+    def added(i, value):
+        remote(over_s.at[i], over_in.at[i], or_send.at[i], or_recv.at[i], plane(i)).wait_recv()
+        return value + over_in[i]
+
+    def arrived(i, carry):
+        gathering_over(i).wait_recv()
+        return carry
+
+    def drain_over(i, carry):
+        remote(over_s.at[lax.rem(e + i, AGG)], over_in.at[i], or_send.at[i], or_recv.at[i], plane(i)).wait_send()
+        gathering_over(i).wait_send()
+        return carry
+
+    lax.fori_loop(1, AGG, scattering, 0)
+    lax.fori_loop(24, AGG - 1, take, 0)
     first, second = [], []
     for kind, rows, copies in ((0, pl.ds(0, HEAD), first), (1, pl.ds(HEAD, ROWS - HEAD), second)):
-        if kind:
-            for copy in over_ys:
-                copy.wait_recv()
-            mine = over_n[...]
-            for i in range(1, 8):
-                mine = mine + over_yin[i]
-            over_g[half] = mine
-            send(over_g.at[half], over_g.at[half], og_send.at[0], og_recv.at[0], at(lax.rem(z + 4, NZ), y, c, x))
         for i in far:
             zz = lax.rem(z + i, NZ)
             copies.append(
                 send(part.at[zz, rows], landed.at[i, rows], a_send.at[kind, i], a_recv.at[kind, i], at(zz, y, c, x))
             )
-    other_half = over_g.at[1 - half]
-    remote(other_half, other_half, og_send.at[0], og_recv.at[0], at(lax.rem(z + 4, NZ), y, c, x)).wait_recv()
+    over_all[e] = lax.fori_loop(1, AGG, added, over_s[e])
+    lax.fori_loop(1, AGG, spreading, 0)
+    lax.fori_loop(1, AGG, arrived, 0)
     bucket = (x * 2 + half) * 8 + y * 2 + c
     owned = full[...] == bucket
     for copy in first:
@@ -278,7 +282,7 @@
 
     def total(g):
         rows = slice(g * 8, g * 8 + 8)
-        value = part[z, rows] + jnp.where(owned, over_g[g // 4, g % 4 * 8 : g % 4 * 8 + 8], 0.0)
+        value = part[z, rows] + jnp.where(owned, jnp.concatenate([over_all[g * 4 + i] for i in range(4)], axis=0), 0.0)
         for i in range(1, NZ):
             value = value + landed[i, rows]
         return value
@@ -295,26 +299,15 @@
 
     for i in (8, 7, 9, 6, 10, 5, 11, 4, 12, 3, 13, 2, 14, 1, 15):
         send(gath.at[a_me], gath.at[a_me], g_send.at[i], g_recv.at[i], gathering(i)[1])
-    owned_blocks[0:8] = mix
+    row_blocks[x, 0:8] = mix
     for copy in second:
         copy.wait_recv()
     for g in range(2, 7):
-        owned_blocks[g * 8 - 8 : g * 8] = total(g)
-    home = x * 2 + half
-    for j in range(1, NX):
-        peer = at(home, y, c, lax.rem(x + j, NX))
-        send(owned_blocks, blocks.at[quarter], b_send.at[j], b_recv.at[quarter], peer)
-
-    def to_home():
-        return remote(owned_blocks, blocks.at[quarter], b_send.at[0], b_recv.at[quarter], at(home, y, c, x))
-
-    @pl.when(home != z)
-    def _():
-        to_home().start()
-
-    @pl.when(home == z)
-    def _():
-        blocks[quarter] = owned_blocks[...]
+        row_blocks[x, g * 8 - 8 : g * 8] = total(g)
+    row = []
+    for i in (1, 3, 2):
+        piece = row_blocks.at[x]
+        row.append(send(piece, piece, b_send.at[i], b_recv.at[i], at(z, y, c, lax.rem(x + i, NX))))
 
     def settle(i, carry):
         a = lax.rem(a_me + 16 - i, 16)
@@ -373,6 +366,23 @@
         for v in (0, 1):
             group = held[v].at[c, p, q]
             send(group, group, m_send.at[v, i], m_recv.at[v, i], cross(p, lax.rem(q + i, 4)))
+    for i in range(1, NX):
+        piece = row_blocks.at[lax.rem(x + NX - i, NX)]
+        remote(piece, piece, b_send.at[i], b_recv.at[i], at(z, y, c, lax.rem(x + i, NX))).wait_recv()
+
+    def homing(k):
+        return remote(row_blocks.at[k], blocks.at[quarter], h_send.at[k], h_recv.at[quarter], at(k * 2 + half, y, c, x))
+
+    for k in range(NX):
+
+        @pl.when(k * 2 + half != z)
+        def _():
+            homing(k).start()
+
+        @pl.when(k * 2 + half == z)
+        def _():
+            blocks[quarter] = row_blocks[k]
+
     for i in (0, 1, 3, 2):
         for v in (0, 1):
             group = held[v].at[c, p, back(q, i)]
@@ -391,16 +401,14 @@
                 put(v, c, back(p, j), back(q, i))
     for k in range(4):
         slot = blocks.at[k]
-        source = lax.rem(z, 2) * 4 + k
-        mine_here = (x == z // 2) & (source == z)
-
-        @pl.when(jnp.logical_not(mine_here))
+
+        @pl.when(lax.rem(z, 2) * 4 + k != z)
         def _():
-            remote(slot, slot, b_send.at[0], b_recv.at[k], at(home, y, c, lax.rem(x + 1, NX))).wait_recv()
-
-    @pl.when(home != z)
-    def _():
-        to_home().wait_send()
+            remote(slot, slot, h_send.at[0], h_recv.at[k], at(lax.rem(z + 1, NZ), y, c, x)).wait_recv()
+
+        @pl.when(k * 2 + half != z)
+        def _():
+            homing(k).wait_send()
 
     out_blocks = pltpu.make_async_copy(blocks, blocks_out, blocks_sem.at[0])
     out_blocks.start()
@@ -411,6 +419,7 @@
                 remote(group, group, p_send.at[v, j, i], p_recv.at[v, j, i], other).wait_recv()
                 put(v, 1 - c, back(q, j), back(p, i))
     lax.fori_loop(0, AGG - 1, drain, 0)
+    lax.fori_loop(1, AGG, drain_over, 0)
     for copy in sent:
         copy.wait_send()
     for copy in outs:
@@ -420,12 +429,11 @@
 
 def write_kernel(all_in, nine_in, blocks_in, gradient_out, blocks_out, held, nine, blocks, gradient, wide, in_sem, out_sem):
     reads = []
-    for k in range(NX * NY):
-        x, y = k // NY, k % NY
+    for k in range(NX):
         for v, (src, dst) in enumerate(((all_in, held), (nine_in, nine))):
-            for c, (p, q) in enumerate(((x, y), (y, x))):
-                reads.append(pltpu.make_async_copy(src.at[c, p, q], dst.at[c, p, q], in_sem.at[k * 4 + v * 2 + c]))
-    last = NX * NY
+            for c, cut in enumerate(((0, k), (1, slice(None), k))):
+                reads.append(pltpu.make_async_copy(src.at[cut], dst.at[cut], in_sem.at[k * 4 + v * 2 + c]))
+    last = NX
     reads.append(pltpu.make_async_copy(blocks_in, blocks, in_sem.at[last * 4]))
     for read in reads:
         read.start()
@@ -448,10 +456,9 @@
     for k in range(last):
         for read in reads[k * 4 : k * 4 + 4]:
             read.wait()
-        x, y = k // NY, k % NY
-        for block in range(16):
-            z, c = block // 2, block % 2
-            p, q = (y, x) if c else (x, y)
+        for block in range(64):
+            y, z, c = block // 16, block // 2 % 8, block % 2
+            p, q = (y, k) if c else (k, y)
             lanes = k * step + block * LOW
             gradient[0:8, lanes : lanes + 128] = held[c, p, q, z, 0:8]
             gradient[0:8, lanes + 128 : lanes + 256] = held[c, p, q, z, 8:16]
@@ -491,7 +498,7 @@
             VMEM((AGG, 2, 21, LIVE), F32),
             VMEM((NZ, ROWS, width), F32),
             VMEM((NZ, ROWS, width), F32),
-            VMEM((KEPT, width), F32),
+            VMEM((NX, KEPT, width), F32),
             VMEM((m, KEPT, width), F32),
             VMEM((16, 18, 128), F32),
             VMEM((16, LOW, width), BF16),
@@ -500,19 +507,16 @@
             VMEM((16, 18, 128), F32),
             VMEM((2, 4, 4, NZ, 16, 128), F32),
             VMEM((2, 4, 4, NZ, 2, 128), F32),
-            VMEM((m, 64, width), F32),
+            VMEM((m, ROWS, width), F32),
             VMEM((21, LIVE), F32),
             VMEM((8, LIVE), jnp.int32),
-            VMEM((NZ, 32, width), F32),
-            VMEM((32, width), F32),
-            VMEM((NX, 32, width), F32),
-            VMEM((32, width), F32),
-            VMEM((8, 32, width), F32),
-            VMEM((2, 32, width), F32),
+            VMEM((NZ, ROWS, width), F32),
+            VMEM((AGG, 2, width), F32),
+            VMEM((AGG, 2, width), F32),
+            VMEM((AGG, 2, width), F32),
         ]
-        + [dma((AGG,))] * 2 + [dma((2, NZ))] * 2 + [dma((4,))] * 2 + [dma((16,))] * 4 + [dma((2, NZ))] * 2 + [dma((2, 4))] * 2
-        + [dma((2, 4, 4))] * 4 + [dma((NZ,))] * 2 + [dma((NX,))] * 2 + [dma((8,))] * 2 + [dma((1,))] * 2
-        + [dma((2, 2, 4, 4)), dma((1,))],
+        + [dma((AGG,))] * 2 + [dma((2, NZ))] * 2 + [dma((4,))] * 4 + [dma((16,))] * 4 + [dma((2, NZ))] * 2 + [dma((2, 4))] * 2
+        + [dma((2, 4, 4))] * 4 + [dma((NZ,))] * 2 + [dma((AGG,))] * 4 + [dma((2, 2, 4, 4)), dma((1,))],
         compiler_params=pltpu.CompilerParams(collective_id=0, has_side_effects=True, vmem_limit_bytes=limit),
     )(bucket_counts, jacobians, residuals, camera_local.reshape(1, slots), camera_map.reshape(1, cams))
     shapes = (jax.ShapeDtypeStruct((9, cams), F32), jax.ShapeDtypeStruct((81, CAM_DEV), F32))
@@ -523,7 +527,7 @@
         out_specs=(anywhere, anywhere),
         scratch_shapes=[
             VMEM(gathered.shape, F32), VMEM(ninth.shape, F32), VMEM(blocks.shape, F32), VMEM(shapes[0].shape, F32),
-            VMEM(shapes[1].shape, F32), dma((NX * NY * 4 + 1,)), dma((NX * NY + 1,)),
+            VMEM(shapes[1].shape, F32), dma((NX * 4 + 1,)), dma((NX + 1,)),
         ],
         compiler_params=pltpu.CompilerParams(vmem_limit_bytes=limit),
     )(gathered, ninth, blocks)

time: 110 us -> 90.4 us (0.82)
  Pallas kernels: 108 us -> 89.6 us
    pallas_call x1, Pallas kernels: 104 us -> 85.5 us  [local(): pl.pallas_call(functools.partial(main_kernel, n, m), out_shape=(jax.Shape...]
where the time goes in v3:
time: 90.4 us; the launch traced here: 90.3 us
  Pallas kernels  89.6 us (99%)
    pallas_call x1, Pallas kernels, local(): pl.pallas_call(functools.partial(main_kernel, n, m), out_shape=(jax.Shape...  85.5 us
    pallas_call x1, Pallas kernels, local(): pl.pallas_call(write_kernel, out_shape=shapes, in_specs=[anywhere] * 3, o...  4.11 us

profile of v3, /device:TPU:1, one launch (start us, length us, event | category | flops | bytes accessed | tf_op | source)
XLA Modules:
  0.0 90.3 jit_solution(4226686616440310279)
XLA Ops:
  0.6 85.5 %shard_map.68 = (f32[2,4,4,8,16,128]{5,4,3,2,1,0:T(8,128)}, f32[2,4,4,8,2,128]{5,4,3,2,1,0:T(2,128)}, f32[4,48,256]{2,1,0:T(8,128)}) custom-call(s32[1,64]{1,0:T(1,128)} %counts.1, f32[18,32768]{1,0:T(8,128)} %jac_in.1, f32[2,32768]{1,0:T(2,128)} %res_in.1, s32[1,32768]{1,0:T(1,128)} %bitcast.3, s32[1,65536]{1,0:T(1,128)} %bitcast.2), custom_call_target="tpu_custom_call" | custom-call | tf_op jit(solution)/shard_map/pallas_call | solution.py:482
  86.2 4.1 %shard_map.69 = (f32[9,65536]{1,0:T(8,128)}, f32[81,1024]{1,0:T(8,128)}) custom-call(f32[2,4,4,8,16,128]{5,4,3,2,1,0:T(8,128)} %get-tuple-element.5.all_in, f32[2,4,4,8,2,128]{5,4,3,2,1,0:T(2,128)} %get-tuple-element.6.nine_in, f32[4,48,256]{2,1,0:T(8,128)} %get-tuple-element.7.blocks_in), custom_call_target="tpu_custom_call" | custom-call | tf_op jit(solution)/shard_map/pallas_call | solution.py:523

commit v4 on v3

--- a/solution.py
+++ b/solution.py
@@ -159,46 +159,6 @@
         found = (jac[:, rest], res[:, rest], late, jnp.full((8, LIVE), d, jnp.int32))
         return tuple(jnp.where(count[0 : new.shape[0]] > LIVE, new, old) for new, old in zip(found, carry))
 
-    pl.semaphore_wait(barrier, len(peers))
-
-    def remote(src, dst, s, r, peer):
-        return pltpu.make_async_remote_copy(
-            src_ref=src, dst_ref=dst, send_sem=s, recv_sem=r, device_id=peer, device_id_type=MESH
-        )
-
-    sent = []
-
-    def send(*args):
-        copy = remote(*args)
-        copy.start()
-        sent.append(copy)
-        return copy
-
-    def handing(k):
-        i = AGG // 2 + (k + 1) // 2 * (1 - 2 * lax.rem(k, 2))
-        return remote(packed.at[lax.rem(e + i, AGG)], moved.at[i], x_send.at[i], x_recv.at[i], plane(i))
-
-    def start(k, carry):
-        i = AGG // 2 + (k + 1) // 2 * (1 - 2 * lax.rem(k, 2))
-        ee = lax.rem(e + i, AGG)
-        pack(ee, 0)
-        pack(ee, 1)
-        handing(k).start()
-        return carry
-
-    def take(k, carry):
-        i = AGG // 2 + (k + 1) // 2 * (1 - 2 * lax.rem(k, 2))
-        handing(k).wait_recv()
-        add_block(moved[i, 0], part.at[0:4])
-        add_block(moved[i, 1], part.at[4:8])
-        return carry
-
-    def drain(k, carry):
-        handing(k).wait_send()
-        return carry
-
-    far = (4, 3, 5, 2, 6, 1, 7)
-    lax.fori_loop(0, 6, start, 0)
     kept = (jnp.zeros((18, LIVE), F32), jnp.zeros((2, LIVE), F32), jnp.full((1, LIVE), -1, F32), jnp.zeros((8, LIVE), jnp.int32))
     kept = lax.fori_loop(0, n, scan, kept, unroll=4)
     over_block[0:18, :] = kept[0]
@@ -206,12 +166,51 @@
     over_block[20:21, :] = kept[2]
     full[...] = kept[3]
     add_block(over_block[...], over)
+    pl.semaphore_wait(barrier, len(peers))
+
+    def remote(src, dst, s, r, peer):
+        return pltpu.make_async_remote_copy(
+            src_ref=src, dst_ref=dst, send_sem=s, recv_sem=r, device_id=peer, device_id_type=MESH
+        )
+
+    sent = []
+
+    def send(*args):
+        copy = remote(*args)
+        copy.start()
+        sent.append(copy)
+        return copy
+
+    def handing(k):
+        i = AGG // 2 + (k + 1) // 2 * (1 - 2 * lax.rem(k, 2))
+        return remote(packed.at[lax.rem(e + i, AGG)], moved.at[i], x_send.at[i], x_recv.at[i], plane(i))
+
+    def start(k, carry):
+        i = AGG // 2 + (k + 1) // 2 * (1 - 2 * lax.rem(k, 2))
+        ee = lax.rem(e + i, AGG)
+        pack(ee, 0)
+        pack(ee, 1)
+        handing(k).start()
+        return carry
+
+    def take(k, carry):
+        i = AGG // 2 + (k + 1) // 2 * (1 - 2 * lax.rem(k, 2))
+        handing(k).wait_recv()
+        add_block(moved[i, 0], part.at[0:4])
+        add_block(moved[i, 1], part.at[4:8])
+        return carry
+
+    def drain(k, carry):
+        handing(k).wait_send()
+        return carry
+
+    far = (4, 3, 5, 2, 6, 1, 7)
 
     over_zs = []
     for i in far:
         zz = lax.rem(z + i, NZ)
         over_zs.append(send(over.at[lax.rem(zz, 4)], over_zin.at[i], oz_send.at[i], oz_recv.at[i], at(zz, y, c, x)))
-    lax.fori_loop(6, AGG - 1, start, 0)
+    lax.fori_loop(0, AGG - 1, start, 0)
     pack(e, 0)
     pack(e, 1)
     add_block(packed[e, 0], part.at[0:4])
@@ -226,7 +225,7 @@
         return carry
 
     lax.fori_loop(0, 16, prepare, 0)
-    lax.fori_loop(0, 24, take, 0)
+    lax.fori_loop(0, 12, take, 0)
     for copy in over_zs:
         copy.wait_recv()
     mine = over[quarter]
@@ -264,7 +263,7 @@
         return carry
 
     lax.fori_loop(1, AGG, scattering, 0)
-    lax.fori_loop(24, AGG - 1, take, 0)
+    lax.fori_loop(12, AGG - 1, take, 0)
     first, second = [], []
     for kind, rows, copies in ((0, pl.ds(0, HEAD), first), (1, pl.ds(HEAD, ROWS - HEAD), second)):
         for i in far:
@@ -300,15 +299,6 @@
     for i in (8, 7, 9, 6, 10, 5, 11, 4, 12, 3, 13, 2, 14, 1, 15):
         send(gath.at[a_me], gath.at[a_me], g_send.at[i], g_recv.at[i], gathering(i)[1])
     row_blocks[x, 0:8] = mix
-    for copy in second:
-        copy.wait_recv()
-    for g in range(2, 7):
-        row_blocks[x, g * 8 - 8 : g * 8] = total(g)
-    row = []
-    for i in (1, 3, 2):
-        piece = row_blocks.at[x]
-        row.append(send(piece, piece, b_send.at[i], b_recv.at[i], at(z, y, c, lax.rem(x + i, NX))))
-
     def settle(i, carry):
         a = lax.rem(a_me + 16 - i, 16)
         place_source(gath[a], cmap[:, owner_lanes(a)] // LOW - a_me * 16, ready[a], spread)
@@ -333,6 +323,14 @@
     for i in (8, 7, 9, 6, 10, 5, 11, 4, 12, 3, 13, 2, 14, 1, 15):
         ss = lax.rem(s_me + i, 16)
         reduced.append(send(shares.at[ss], got.at[i], r_send.at[i], r_recv.at[i], at(ss // 2, y, lax.rem(ss, 2), x)))
+    for copy in second:
+        copy.wait_recv()
+    for g in range(2, 7):
+        row_blocks[x, g * 8 - 8 : g * 8] = total(g)
+    row = []
+    for i in (1, 3, 2):
+        piece = row_blocks.at[x]
+        row.append(send(piece, piece, b_send.at[i], b_recv.at[i], at(z, y, c, lax.rem(x + i, NX))))
     for copy in reduced:
         copy.wait_recv()
     value = shares[s_me]
@@ -428,13 +426,12 @@
 
 
 def write_kernel(all_in, nine_in, blocks_in, gradient_out, blocks_out, held, nine, blocks, gradient, wide, in_sem, out_sem):
-    reads = []
-    for k in range(NX):
-        for v, (src, dst) in enumerate(((all_in, held), (nine_in, nine))):
-            for c, cut in enumerate(((0, k), (1, slice(None), k))):
-                reads.append(pltpu.make_async_copy(src.at[cut], dst.at[cut], in_sem.at[k * 4 + v * 2 + c]))
-    last = NX
-    reads.append(pltpu.make_async_copy(blocks_in, blocks, in_sem.at[last * 4]))
+    last = NX * 2
+    reads = [pltpu.make_async_copy(blocks_in, blocks, in_sem.at[0]), pltpu.make_async_copy(nine_in, nine, in_sem.at[1])]
+    for k in range(last):
+        x, some = k // 2, pl.ds(k % 2 * 2, 2)
+        reads.append(pltpu.make_async_copy(all_in.at[0, x, some], held.at[0, x, some], in_sem.at[2 + k * 2]))
+        reads.append(pltpu.make_async_copy(all_in.at[1, some, x], held.at[1, some, x], in_sem.at[3 + k * 2]))
     for read in reads:
         read.start()
     step = gradient.shape[1] // last
@@ -445,7 +442,7 @@
         copy.start()
         writes.append(copy)
 
-    reads[last * 4].wait()
+    reads[0].wait()
     pieces, _, width = blocks.shape
     for k in range(9):
         for l in range(9):
@@ -453,12 +450,14 @@
             for r in range(pieces):
                 wide[k * 9 + l : k * 9 + l + 1, r * width : (r + 1) * width] = blocks[r, row : row + 1, :]
     write(wide, blocks_out, last)
+    reads[1].wait()
     for k in range(last):
-        for read in reads[k * 4 : k * 4 + 4]:
+        for read in reads[2 + k * 2 : 4 + k * 2]:
             read.wait()
-        for block in range(64):
-            y, z, c = block // 16, block // 2 % 8, block % 2
-            p, q = (y, k) if c else (k, y)
+        x = k // 2
+        for block in range(32):
+            y, z, c = k % 2 * 2 + block // 16, block // 2 % 8, block % 2
+            p, q = (y, x) if c else (x, y)
             lanes = k * step + block * LOW
             gradient[0:8, lanes : lanes + 128] = held[c, p, q, z, 0:8]
             gradient[0:8, lanes + 128 : lanes + 256] = held[c, p, q, z, 8:16]
@@ -527,7 +526,7 @@
         out_specs=(anywhere, anywhere),
         scratch_shapes=[
             VMEM(gathered.shape, F32), VMEM(ninth.shape, F32), VMEM(blocks.shape, F32), VMEM(shapes[0].shape, F32),
-            VMEM(shapes[1].shape, F32), dma((NX * 4 + 1,)), dma((NX + 1,)),
+            VMEM(shapes[1].shape, F32), dma((NX * 4 + 2,)), dma((NX * 2 + 1,)),
         ],
         compiler_params=pltpu.CompilerParams(vmem_limit_bytes=limit),
     )(gathered, ninth, blocks)

time: 90.4 us -> 86.7 us (0.959)
  Pallas kernels: 89.6 us -> 85.9 us
    pallas_call x1, Pallas kernels: 85.5 us -> 82.5 us  [local(): pl.pallas_call(functools.partial(main_kernel, n, m), out_shape=(jax.Shape...]
where the time goes in v4:
time: 86.7 us; the launch traced here: 86.5 us
  Pallas kernels  85.9 us (99%)
    pallas_call x1, Pallas kernels, local(): pl.pallas_call(functools.partial(main_kernel, n, m), out_shape=(jax.Shape...  82.5 us
    pallas_call x1, Pallas kernels, local(): pl.pallas_call(write_kernel, out_shape=shapes, in_specs=[anywhere] * 3, o...  3.42 us

profile of v4, /device:TPU:1, one launch (start us, length us, event | category | flops | bytes accessed | tf_op | source)
XLA Modules:
  0.0 86.5 jit_solution(5521397954201879584)
XLA Ops:
  0.6 82.5 %shard_map.68 = (f32[2,4,4,8,16,128]{5,4,3,2,1,0:T(8,128)}, f32[2,4,4,8,2,128]{5,4,3,2,1,0:T(2,128)}, f32[4,48,256]{2,1,0:T(8,128)}) custom-call(s32[1,64]{1,0:T(1,128)} %counts.1, f32[18,32768]{1,0:T(8,128)} %jac_in.1, f32[2,32768]{1,0:T(2,128)} %res_in.1, s32[1,32768]{1,0:T(1,128)} %bitcast.3, s32[1,65536]{1,0:T(1,128)} %bitcast.2), custom_call_target="tpu_custom_call" | custom-call | tf_op jit(solution)/shard_map/pallas_call | solution.py:481
  83.1 3.4 %shard_map.69 = (f32[9,65536]{1,0:T(8,128)}, f32[81,1024]{1,0:T(8,128)}) custom-call(f32[2,4,4,8,16,128]{5,4,3,2,1,0:T(8,128)} %get-tuple-element.5.all_in, f32[2,4,4,8,2,128]{5,4,3,2,1,0:T(2,128)} %get-tuple-element.6.nine_in, f32[4,48,256]{2,1,0:T(8,128)} %get-tuple-element.7.blocks_in), custom_call_target="tpu_custom_call" | custom-call | tf_op jit(solution)/shard_map/pallas_call | solution.py:522

commit v5 on v4

--- a/solution.py
+++ b/solution.py
@@ -225,7 +225,7 @@
         return carry
 
     lax.fori_loop(0, 16, prepare, 0)
-    lax.fori_loop(0, 12, take, 0)
+    lax.fori_loop(0, 10, take, 0)
     for copy in over_zs:
         copy.wait_recv()
     mine = over[quarter]
@@ -263,7 +263,7 @@
         return carry
 
     lax.fori_loop(1, AGG, scattering, 0)
-    lax.fori_loop(12, AGG - 1, take, 0)
+    lax.fori_loop(10, AGG - 1, take, 0)
     first, second = [], []
     for kind, rows, copies in ((0, pl.ds(0, HEAD), first), (1, pl.ds(HEAD, ROWS - HEAD), second)):
         for i in far:
@@ -343,10 +343,19 @@
         for v in (0, 1):
             own = held[v].at[c, p, q, z]
             send(own, own, z_send.at[v, i], z_recv.at[v, i], at(lax.rem(z + i, NZ), y, c, x))
-    for i in range(1, NZ):
+    def onward(v, src):
+        for i in (1, 3, 2):
+            remote(src, src, m_send.at[v, i], m_recv.at[v, i], cross(p, lax.rem(q + i, 4))).start()
+            remote(src, src, l_send.at[v, i, 0], l_recv.at[v, i, 0], cross(lax.rem(p + i, 4), q)).start()
+
+    onward(0, every.at[c, p, q, z])
+    for i in (1, 7, 2, 6, 3, 5, 4):
         for v in (0, 1):
             slot = held[v].at[c, p, q, lax.rem(z + NZ - i, NZ)]
             remote(slot, slot, z_send.at[v, i], z_recv.at[v, i], at(lax.rem(z + i, NZ), y, c, x)).wait_recv()
+            if v == 0:
+                onward(0, slot)
+    onward(1, nine.at[c, p, q])
     outs = []
 
     def put(v, cc, pp, qq):
@@ -360,10 +369,6 @@
     def back(v, i):
         return lax.rem(v + 4 - i, 4)
 
-    for i in (1, 3, 2):
-        for v in (0, 1):
-            group = held[v].at[c, p, q]
-            send(group, group, m_send.at[v, i], m_recv.at[v, i], cross(p, lax.rem(q + i, 4)))
     for i in range(1, NX):
         piece = row_blocks.at[lax.rem(x + NX - i, NX)]
         remote(piece, piece, b_send.at[i], b_recv.at[i], at(z, y, c, lax.rem(x + i, NX))).wait_recv()
@@ -386,8 +391,9 @@
             group = held[v].at[c, p, back(q, i)]
             if i:
                 remote(group, group, m_send.at[v, i], m_recv.at[v, i], cross(p, lax.rem(q + i, 4))).wait_recv()
-            for j in (1, 3, 2):
-                send(group, group, l_send.at[v, j, i], l_recv.at[v, j, i], cross(lax.rem(p + j, 4), q))
+            if i:
+                for j in (1, 3, 2):
+                    send(group, group, l_send.at[v, j, i], l_recv.at[v, j, i], cross(lax.rem(p + j, 4), q))
             send(group, group, p_send.at[v, 0, i], p_recv.at[v, 0, i], other)
             put(v, c, p, back(q, i))
     for i in (0, 1, 3, 2):
@@ -416,6 +422,11 @@
                 group = held[v].at[1 - c, back(q, j), back(p, i)]
                 remote(group, group, p_send.at[v, j, i], p_recv.at[v, j, i], other).wait_recv()
                 put(v, 1 - c, back(q, j), back(p, i))
+    for v in (0, 1):
+        group = held[v].at[c, p, q]
+        for i in (1, 3, 2):
+            remote(group, group, m_send.at[v, i], m_recv.at[v, i], cross(p, lax.rem(q + i, 4))).wait_send()
+            remote(group, group, l_send.at[v, i, 0], l_recv.at[v, i, 0], cross(lax.rem(p + i, 4), q)).wait_send()
     lax.fori_loop(0, AGG - 1, drain, 0)
     lax.fori_loop(1, AGG, drain_over, 0)
     for copy in sent:

time: 86.7 us -> 85 us (0.980)
  Pallas kernels: 85.9 us -> 84.2 us
    pallas_call x1, Pallas kernels: 82.5 us -> 80.8 us  [local(): pl.pallas_call(functools.partial(main_kernel, n, m), out_shape=(jax.Shape...]
where the time goes in v5:
time: 85 us; the launch traced here: 84.8 us
  Pallas kernels  84.2 us (99%)
    pallas_call x1, Pallas kernels, local(): pl.pallas_call(functools.partial(main_kernel, n, m), out_shape=(jax.Shape...  80.8 us
    pallas_call x1, Pallas kernels, local(): pl.pallas_call(write_kernel, out_shape=shapes, in_specs=[anywhere] * 3, o...  3.42 us

profile of v5, /device:TPU:1, one launch (start us, length us, event | category | flops | bytes accessed | tf_op | source)
XLA Modules:
  0.0 84.8 jit_solution(16094344241743865922)
XLA Ops:
  0.6 80.8 %shard_map.68 = (f32[2,4,4,8,16,128]{5,4,3,2,1,0:T(8,128)}, f32[2,4,4,8,2,128]{5,4,3,2,1,0:T(2,128)}, f32[4,48,256]{2,1,0:T(8,128)}) custom-call(s32[1,64]{1,0:T(1,128)} %counts.1, f32[18,32768]{1,0:T(8,128)} %jac_in.1, f32[2,32768]{1,0:T(2,128)} %res_in.1, s32[1,32768]{1,0:T(1,128)} %bitcast.3, s32[1,65536]{1,0:T(1,128)} %bitcast.2), custom_call_target="tpu_custom_call" | custom-call | tf_op jit(solution)/shard_map/pallas_call | solution.py:492
  81.4 3.4 %shard_map.69 = (f32[9,65536]{1,0:T(8,128)}, f32[81,1024]{1,0:T(8,128)}) custom-call(f32[2,4,4,8,16,128]{5,4,3,2,1,0:T(8,128)} %get-tuple-element.5.all_in, f32[2,4,4,8,2,128]{5,4,3,2,1,0:T(2,128)} %get-tuple-element.6.nine_in, f32[4,48,256]{2,1,0:T(8,128)} %get-tuple-element.7.blocks_in), custom_call_target="tpu_custom_call" | custom-call | tf_op jit(solution)/shard_map/pallas_call | solution.py:533
